TPU v7x, 128 devices: a whole 4x4x4 slice. The times are simulated.
128 devices in a mesh: rep: 4 (over y_hi, core), grp: 32 (over y_lo, x, z).
Axes of the slice: x: 4, y: 4 (y_hi: 2, y_lo: 2; y = y_hi * 2 + y_lo), z: 4, core: 2. Of those that a mesh axis runs over, the one named last changes fastest.
Arguments:
- hidden_in: bfloat16 [512, 7168], P(('rep', 'grp')), may hold values from -3 to 3
- q_nope: bfloat16 [512, 8192], P(('rep', 'grp')), may hold values from -9 to 9
- q_rope: bfloat16 [512, 4096], P(('rep', 'grp')), may hold values from -36 to 36
- new_kv: bfloat16 [512, 576], P(('rep', 'grp')), may hold values from -6 to 6
- cache_kv: bfloat16 [512, 4096, 576], P(('rep', 'grp')), may hold values from -10 to 10
- lengths: int32 [512], P(('rep', 'grp')), may hold values from 2 to 4096, as said below
- w_uk: bfloat16 [512, 8192], P('rep'), may hold values from -0.5 to 0.5
- w_uv: bfloat16 [512, 8192], P('rep'), may hold values from -0.25 to 0.25
- w_out: bfloat16 [8192, 7168], P('grp'), may hold values from -0.0625 to 0.0625
- norm_gain: bfloat16 [7168], replicated, may hold values from 0.5 to 1.5
- w_gate: bfloat16 [7168, 18432], P(None, ('rep', 'grp')), may hold values from -0.0625 to 0.0625
- w_up: bfloat16 [7168, 18432], P(None, ('rep', 'grp')), may hold values from -0.0625 to 0.0625
- w_down: bfloat16 [18432, 7168], P(('rep', 'grp')), may hold values from -0.046875 to 0.046875
Outputs:
- hidden_out: bfloat16 [512, 7168], P(('rep', 'grp'))
Inputs may be any that keep to these rules, and one draw needn't show every extreme that they name: `lengths`: every sequence has 2 or more cached positions and at most 4096; some sequence has exactly 4096.
All inputs are finite; a program needn't handle non-finite values.
Results may differ from a plain program's by a relative error of at most 0.03.
Values may be sent and summed in bfloat16 or wider, within the bound.
A program may use at most 192 MiB of HBM per device.

v0:
```python
import jax
import jax.numpy as jnp
from jax import lax
from jax.sharding import PartitionSpec as P

H = 64
NOPE = 128
ROPE = 64
VH = 128
KV_RANK = 512
CACHE = 4096


epsilon = 1e-06


def in_one_piece(arrays, axis, dim, along):
    ends, at = ([], 0)
    for a in arrays[:-1]:
        at += a.shape[along]
        ends.append(at)
    both = jnp.concatenate(arrays, axis=along)
    return tuple(jnp.split(lax.all_gather(both, axis, axis=dim, tiled=True), ends, axis=along))


def norm_rows(resid, norm_gain):
    resid_f32 = resid.astype(jnp.float32)
    mean_sq = jnp.mean(resid_f32 * resid_f32, axis=1, keepdims=True)
    return (resid_f32 * lax.rsqrt(mean_sq + epsilon) * norm_gain.astype(jnp.float32)).astype(
        jnp.bfloat16
    )


def gated_rows(rows_in, gate_cols, up_cols):
    gate_val = jnp.dot(rows_in, gate_cols, preferred_element_type=jnp.float32)
    up_val = jnp.dot(rows_in, up_cols, preferred_element_type=jnp.float32)
    return (jax.nn.silu(gate_val) * up_val).astype(jnp.bfloat16)


def on_device(
    hidden_in,
    q_nope,
    q_rope,
    new_kv,
    cache_kv,
    lengths,
    w_uk,
    w_uv,
    w_out,
    norm_gain,
    w_gate,
    w_up,
    w_down,
):
    seq_count = hidden_in.shape[0]
    key_up, value_up = in_one_piece((w_uk, w_uv), "rep", 0, 1)
    nope_part = q_nope.reshape(seq_count, H, NOPE)
    q_lat = jnp.einsum(
        "bhd,chd->bhc",
        nope_part,
        key_up.reshape(KV_RANK, H, NOPE),
        preferred_element_type=jnp.float32,
    ).astype(jnp.bfloat16)
    queries = jnp.concatenate([q_lat, q_rope.reshape(seq_count, H, ROPE)], axis=2)
    score_scale = float(NOPE + ROPE) ** (-0.5)
    scores = (
        jnp.einsum("bhc,blc->bhl", queries, cache_kv, preferred_element_type=jnp.float32)
        * score_scale
    )
    positions = lax.broadcasted_iota(jnp.int32, (1, 1, CACHE), 2)
    scores = jnp.where(positions < lengths[:, None, None], scores, -jnp.inf)
    own_score = (
        jnp.einsum("bhc,bc->bh", queries, new_kv, preferred_element_type=jnp.float32) * score_scale
    )
    row_top = jnp.maximum(jnp.max(scores, axis=2), own_score)
    weights = jnp.exp(scores - row_top[:, :, None])
    own_weight = jnp.exp(own_score - row_top)
    denom_sum = jnp.sum(weights, axis=2) + own_weight
    softmax_w = (weights / denom_sum[:, :, None]).astype(jnp.bfloat16)
    own_prob = (own_weight / denom_sum).astype(jnp.bfloat16)
    mixture = jnp.einsum("bhl,blc->bhc", softmax_w, cache_kv, preferred_element_type=jnp.float32)
    mixture = (
        mixture + own_prob.astype(jnp.float32)[:, :, None] * new_kv.astype(jnp.float32)[:, None, :]
    )
    latent = mixture[:, :, :KV_RANK].astype(jnp.bfloat16)
    head_out = jnp.einsum(
        "bhc,che->bhe", latent, value_up.reshape(KV_RANK, H, VH), preferred_element_type=jnp.float32
    ).astype(jnp.bfloat16)
    regrouped = lax.all_to_all(head_out, "grp", split_axis=1, concat_axis=0, tiled=True)
    group_count = regrouped.shape[0]
    partial_value = jnp.dot(
        regrouped.reshape(group_count, -1), w_out, preferred_element_type=jnp.float32
    )
    offset = lax.axis_index("grp") * seq_count
    own_part = lax.dynamic_slice_in_dim(partial_value, offset, seq_count, 0) + hidden_in.astype(
        jnp.float32
    )
    partial_value = lax.dynamic_update_slice_in_dim(partial_value, own_part, offset, 0)
    summed = lax.psum(partial_value.astype(jnp.bfloat16), "grp")
    normed_group = norm_rows(summed, norm_gain)
    resid_own = lax.dynamic_slice_in_dim(summed, offset, seq_count, 0)
    every_row = lax.all_gather(normed_group, "rep", axis=0, tiled=True)
    activated = gated_rows(every_row, w_gate, w_up)
    mlp_out = lax.psum_scatter(
        jnp.dot(activated, w_down, preferred_element_type=jnp.float32),
        ("rep", "grp"),
        scatter_dimension=0,
        tiled=True,
    )
    return (resid_own.astype(jnp.float32) + mlp_out).astype(jnp.bfloat16)


def solution(mesh):
    return jax.shard_map(
        on_device,
        mesh=mesh,
        in_specs=(
            P(("rep", "grp"), None),
            P(("rep", "grp"), None),
            P(("rep", "grp"), None),
            P(("rep", "grp"), None),
            P(("rep", "grp"), None, None),
            P(("rep", "grp")),
            P("rep", None),
            P("rep", None),
            P("grp", None),
            P(),
            P(None, ("rep", "grp")),
            P(None, ("rep", "grp")),
            P(("rep", "grp"), None),
        ),
        out_specs=P(("rep", "grp"), None),
        check_vma=False,
    )
```

profile of v0, /device:TPU:0, one launch (start us, length us, event | category | flops | bytes accessed | tf_op | source)
XLA Modules:
  0.0 765.4 jit_solution(8639748796837083313)
XLA Ops:
  6.5 4.2 copy.26
  10.7 4.1 copy.27
  14.8 5.6 pad_maximum_fusion
  20.5 0.7 copy-done.3
  21.5 113.8 %all-gather.3.cloned.1.call-done = bf16[512,16384]{0,1:T(8,128)(2,1)} async-done(((bf16[128,16384]{0,1:T(8,128)(2,1)}), bf16[512,16384]{0,1:T(8,128)(2,1)}) %all-gather.3.cloned.1.call-update) | async-done | bytes 16777232 | tf_op jit(solution)/shard_map/all_gather | solution.py:23
  135.3 9.1 %fusion.32 = (bf16[512,8192]{0,1:T(8,128)(2,1)S(1)}, bf16[512,8192]{0,1:T(8,128)(2,1)}) fusion(bf16[512,16384]{0,1:T(8,128)(2,1)} %all-gather.3.cloned.1.call-done), kind=kLoop, calls=%fused_computation.50 | loop fusion | bytes 33554432 | tf_op jit(solution)/shard_map/split | solution.py:23
  144.4 1.2 fusion.8
  145.9 8.4 %fusion.33 = (f32[4,64]{1,0:T(4,128)S(1)}, f32[4,64,4096]{2,1,0:T(8,128)S(1)}) fusion(bf16[4,4096,576]{1,2,0:T(8,128)(2,1)} %param.17, bf16[4,64,576]{2,0,1:T(4,128)(2,1)S(1)} %pad_maximum_fusion.1, pred[4,4096]{1,0:T(4,128)(4,1)S(1)} %iota_compare_fusion), kind=kOutput, calls=%fused_computation.51 | convolution fusion | flops 1211105024 | bytes 23380992 | tf_op jit(solution)/shard_map/bhc,blc->bhl/dot_general | solution.py:67
  154.4 0.7 fusion.1
  155.1 9.6 %fusion.5 = f32[4,64,576]{2,1,0:T(8,128)S(1)} fusion(bf16[4,4096,576]{1,2,0:T(8,128)(2,1)} %param.17, f32[4,64,4096]{2,1,0:T(8,128)S(1)} %get-tuple-element.10, f32[4,64]{1,0:T(4,128)S(1)} %get-tuple-element.8, f32[4,64]{1,0:T(4,128)S(1)} %multiply_maximum_fusion), kind=kOutput, calls=%fused_computation.11 | convolution fusion | flops 1211105280 | bytes 23660544 | tf_op jit(solution)/shard_map/bhl,blc->bhc/dot_general | solution.py:81
  164.8 6.3 fusion.11
  171.1 7.4 all-to-all-start
  178.6 8.3 %all-to-all-done = bf16[4,64,128]{2,0,1:T(4,128)(2,1)S(1)} async-done(((bf16[4,64,128]{2,0,1:T(4,128)(2,1)}), bf16[4,64,128]{2,0,1:T(4,128)(2,1)S(1)}, u32[]{:S(2)}, u32[]{:S(2)}) %all-to-all-start) | async-done | bytes 65568 | tf_op jit(solution)/shard_map/all_to_all | solution.py:89
  186.9 2.7 fusion.24
  189.7 1.5 convert_element_type.58
  191.3 310.3 %all-reduce.4.cloned.1.call-done = bf16[128,7168]{1,0:T(8,128)(2,1)} async-done(((bf16[128,7168]{1,0:T(8,128)(2,1)}), bf16[128,7168]{1,0:T(8,128)(2,1)}) %all-reduce.4.cloned.1.call-update) | async-done | bytes 1835024 | tf_op jit(solution)/shard_map/psum | solution.py:99
  501.6 1.9 fusion.2
  503.5 3.3 fusion.4
  506.9 0.2 all-reduce.6.cloned.1.call-start
  507.1 56.6 %all-gather.5.cloned.1.call-done = bf16[512,7168]{1,0:T(8,128)(2,1)} async-done(((bf16[128,7168]{1,0:T(8,128)(2,1)}), bf16[512,7168]{1,0:T(8,128)(2,1)}) %all-gather.5.cloned.1.call-update) | async-done | bytes 7340048 | tf_op jit(solution)/shard_map/all_gather | solution.py:102
  563.6 6.2 fusion.34
  569.9 13.5 %fusion.10 = f32[512,7168]{1,0:T(8,128)} fusion(bf16[144,7168]{1,0:T(8,128)(2,1)S(1)} %copy-done, bf16[512,7168]{1,0:T(8,128)(2,1)} %all-gather.5.cloned.1.call-done, bf16[7168,144]{0,1:T(8,128)(2,1)} %param.24, f32[512,144]{0,1:T(8,128)S(1)} %fusion.34), kind=kOutput, calls=%fused_computation.18 | convolution fusion | flops 2114371584 | bytes 26443776 | tf_op jit(solution)/shard_map/dot_general | solution.py:105
  583.4 173.8 %all-reduce.6.cloned.1.call-done = f32[512,7168]{1,0:T(8,128)} async-done(((f32[512,7168]{1,0:T(8,128)}), f32[512,7168]{1,0:T(8,128)}) %all-reduce.6.cloned.1.call-update) | async-done | bytes 14680080
  757.2 1.7 fusion.23
  (33 shorter events, 1.1 us)
Async XLA Ops:
  6.5 563.4 %copy-start = (bf16[144,7168]{1,0:T(8,128)(2,1)S(1)}, bf16[144,7168]{1,0:T(8,128)(2,1)}, u32[]{:S(2)}) copy-start(bf16[144,7168]{1,0:T(8,128)(2,1)} %param.25) | copy-start | bytes 6193156
  6.5 128.8 %all-gather.3.cloned.1.call-start = ((), (), s32[]{:S(2)}) async-start(), calls=%async_computation.1 | async-start | bytes 20971520 | tf_op jit(solution)/shard_map/all_gather | solution.py:23
  20.4 0.8 copy-start.3
  20.4 0.9 copy-start.5
  20.4 1.0 copy-start.6
  21.5 122.9 %copy-start.1 = (bf16[4,8192]{1,0:T(4,128)(2,1)S(1)}, bf16[4,8192]{1,0:T(4,128)(2,1)}, u32[]{:S(2)}) copy-start(bf16[4,8192]{1,0:T(4,128)(2,1)} %param.14) | copy-start | bytes 196612
  171.1 18.5 %copy-start.2 = (bf16[4,7168]{1,0:T(4,128)(2,1)S(1)}, bf16[4,7168]{1,0:T(4,128)(2,1)}, u32[]{:S(2)}) copy-start(bf16[4,7168]{1,0:T(4,128)(2,1)} %param.13) | copy-start | bytes 172036
  171.1 15.7 %all-to-all-start = ((bf16[4,64,128]{2,0,1:T(4,128)(2,1)}), bf16[4,64,128]{2,0,1:T(4,128)(2,1)S(1)}, u32[]{:S(2)}, u32[]{:S(2)}) async-start(bf16[4,64,128]{2,0,1:T(4,128)(2,1)} %fusion.11), calls=%async_computation | async-start | bytes 131072 | tf_op jit(solution)/shard_map/all_to_all | solution.py:89
  178.5 323.1 %all-reduce.4.cloned.1.call-start = ((), (), s32[]{:S(2)}) async-start(), calls=%async_computation.2 | async-start | bytes 3670016 | tf_op jit(solution)/shard_map/psum | solution.py:99
  189.6 1.6 copy-start.4
  191.2 372.5 %all-gather.5.cloned.1.call-start = ((), (), s32[]{:S(2)}) async-start(), calls=%async_computation.3 | async-start | bytes 9175040 | tf_op jit(solution)/shard_map/all_gather | solution.py:102
  506.9 250.4 %all-reduce.6.cloned.1.call-start = ((), (), s32[]{:S(2)}) async-start(), calls=%async_computation.4 | async-start | bytes 29360128
Sparse Core Ops, SparseCore 0:
  20.6 114.6 all-gather.2
  191.3 310.2 all-reduce.3
  507.0 56.6 all-gather.4
  583.6 173.6 all-reduce.5
where the time goes:
time: 767 us; the launch traced here: 765 us
  waiting for transfers between devices  663 us (86%)
  matrix products  48.1 us (6%)
  local copies, waits for them, and re-layouts  18.3 us (2%)
  other arithmetic  15.2 us (2%)
  between operations  13.3 us (2%)
  starting transfers between devices  7.71 us (1%)
    psum x1, waiting for transfers between devices, on_device(): summed = lax.psum(partial_value.astype(jnp.bfloat16), 'grp')  310 us
    unnamed x5, waiting for transfers between devices  174 us
    all_gather x1, waiting for transfers between devices, in_one_piece(): lax.all_gather(both, axis, axis=dim, tiled=True)  114 us
    all_gather x1, waiting for transfers between devices, on_device(): every_row = lax.all_gather(normed_group, 'rep', axis=0, tiled=True)  56.6 us
  transfers between devices with their start and end apart: 5, of which 5 were waited for; matrix products, arithmetic and copies ran while one was open for 0% of the time, Pallas kernels for 0%

commit v1 on v0

v1 whole, which is shorter than its diff:
```python
import functools

import jax
import jax.numpy as jnp
from jax import lax
from jax.experimental import pallas as pl
from jax.experimental.pallas import tpu as pltpu
from jax.sharding import PartitionSpec as P

D = 7168
FF_OWN = 144
H = 64
NOPE = 128
ROPE = 64
VH = 128
KV_RANK = 512
CACHE = 4096
SEQ = 4
BLOCK = 1024
EPS = 1e-06
SCALE = float(NOPE + ROPE) ** (-0.5)
MESH = pl.DeviceIdType.MESH
F32 = jnp.float32
BF16 = jnp.bfloat16
NT = (((1,), (1,)), ((), ()))
VMEM_LIMIT = 62 * 1024 * 1024


def coordinates():
    r, g = lax.axis_index("rep"), lax.axis_index("grp")
    return dict(
        r=r, g=g, core=r % 2, y=(r // 2) * 2 + g // 16, x=(g // 4) % 4, z=g % 4
    )


def device_at(at, **moved):
    x, y, z = (moved.get(k, at[k]) for k in "xyz")
    return ((y // 2) * 2 + at["core"], ((y % 2) * 4 + x) * 4 + z)


class Copies:
    def __init__(self, send_sems, recv_sems):
        self.send, self.recv, self.used, self.all = send_sems, recv_sems, 0, []

    def start(self, src, dst, device):
        k = self.used
        self.used += 1
        copy = pltpu.make_async_remote_copy(
            src_ref=src,
            dst_ref=dst,
            send_sem=self.send.at[k],
            recv_sem=self.recv.at[k],
            device_id=device,
            device_id_type=MESH,
        )
        copy.start()
        self.all.append(copy)
        return copy

    def finish(self):
        for copy in self.all:
            copy.wait_send()


def barrier_with(peers):
    sem = pltpu.get_barrier_semaphore()
    for peer in peers:
        pl.semaphore_signal(sem, inc=1, device_id=peer, device_id_type=MESH)
    pl.semaphore_wait(sem, len(peers))


class GatherRing:
    def __init__(self, copies, block, me, left, right, cut):
        self.copies, self.block, self.me = copies, block, me
        self.left, self.right, self.cut = left, right, cut

    def go(self, j, half, device):
        ref = self.block(j, self.cut[half])
        return self.copies.start(ref, ref, device)

    def start(self):
        m = self.me
        self.ra = self.go(m, 0, self.right)
        self.lb = self.go(m, 1, self.left)
        self.rb = self.go(m, 1, self.right)
        self.la = self.go(m, 0, self.left)

    def middle(self):
        m = self.me
        self.ra.wait_recv()
        self.rf = self.go((m + 3) % 4, 0, self.right)
        self.lb.wait_recv()
        self.lf = self.go((m + 1) % 4, 1, self.left)

    def end(self):
        for copy in (self.rb, self.la, self.rf, self.lf):
            copy.wait_recv()


class ScatterRing:
    def __init__(self, copies, src, landing, passing, me, left, right, cut):
        self.copies, self.src, self.landing, self.passing = copies, src, landing, passing
        self.me, self.left, self.right, self.cut = me, left, right, cut

    def part(self, j, half):
        start, size = self.cut[half]
        return self.src.at[j, :, pl.ds(start, size)]

    def land(self, k, half):
        return self.landing.at[k, :, pl.ds(0, self.cut[half][1])]

    def start(self):
        m, go = self.me, self.copies.start
        self.r0 = go(self.part((m + 2) % 4, 0), self.land(0, 0), self.right)
        self.l0 = go(self.part((m + 2) % 4, 1), self.land(1, 1), self.left)
        self.r1 = go(self.part((m + 1) % 4, 1), self.land(2, 1), self.right)
        self.l1 = go(self.part((m + 3) % 4, 0), self.land(3, 0), self.left)

    def value(self, ref):
        return ref[...].astype(F32)

    def middle(self):
        m, go = self.me, self.copies.start
        self.r0.wait_recv()
        held = self.passing.at[0, :, pl.ds(0, self.cut[0][1])]
        held[...] = (self.value(self.part((m + 1) % 4, 0)) + self.value(self.land(0, 0))).astype(BF16)
        self.r2 = go(held, self.land(4, 0), self.right)
        self.l0.wait_recv()
        held = self.passing.at[1, :, pl.ds(0, self.cut[1][1])]
        held[...] = (self.value(self.part((m + 3) % 4, 1)) + self.value(self.land(1, 1))).astype(BF16)
        self.l2 = go(held, self.land(5, 1), self.left)

    def end(self):
        m = self.me
        self.l1.wait_recv()
        self.r2.wait_recv()
        first = self.value(self.part(m, 0)) + self.value(self.land(4, 0)) + self.value(self.land(3, 0))
        self.r1.wait_recv()
        self.l2.wait_recv()
        second = self.value(self.part(m, 1)) + self.value(self.land(2, 1)) + self.value(self.land(5, 1))
        return first, second


def query_kernel(q_ref, wuk_ref, wuv_ref, out_ref, wuv_out, gathered, rows, made, own_sem, send_sems, recv_sems):
    at = coordinates()
    r, g = at["r"], at["g"]
    peers = [((r + k) % 4, g) for k in (1, 2, 3)]
    barrier_with(peers)
    copies = Copies(send_sems, recv_sems)
    mine = wuv_ref.at[:, pl.ds(pl.multiple_of(g * 256, 256), 256)]
    incoming = [copies.start(q_ref, gathered.at[r], peer) for peer in peers]
    own = pltpu.make_async_copy(mine, wuv_out.at[r], own_sem)
    own.start()
    weights = [copies.start(mine, wuv_out.at[r], peer) for peer in peers]
    gathered[r] = q_ref[...]
    for copy in incoming:
        copy.wait_recv()
    for s in range(4):
        rows[pl.ds(4 * s, 4), :] = gathered[s].astype(F32)

    def heads(i, carry):
        for k in range(8):
            h = i * 8 + k
            cols = pl.ds(pl.multiple_of(h * NOPE, NOPE), NOPE)
            lat = lax.dot_general(
                rows[:, cols].astype(BF16), wuk_ref[:, cols], NT, preferred_element_type=F32
            )
            for s in range(4):
                made[s, h] = lat[4 * s : 4 * s + 4].astype(BF16)
        return carry

    lax.fori_loop(0, H // 8, heads, 0)
    back = [copies.start(made.at[peer[0]], out_ref.at[r], peer) for peer in peers]
    out_ref[r] = made[r]
    for copy in back + weights:
        copy.wait_recv()
    own.wait()
    copies.finish()


def spread_queries(q_nope, w_uk, w_uv):
    return pl.pallas_call(
        query_kernel,
        out_shape=(
            jax.ShapeDtypeStruct((4, H, SEQ, NOPE), BF16),
            jax.ShapeDtypeStruct((4, 128, 256), BF16),
        ),
        in_specs=[
            pl.BlockSpec(memory_space=pltpu.VMEM),
            pl.BlockSpec(memory_space=pltpu.VMEM),
            pl.BlockSpec(memory_space=pl.ANY),
        ],
        out_specs=(
            pl.BlockSpec(memory_space=pltpu.VMEM),
            pl.BlockSpec(memory_space=pl.ANY),
        ),
        scratch_shapes=[
            pltpu.VMEM((4, SEQ, H * NOPE), BF16),
            pltpu.VMEM((16, H * NOPE), F32),
            pltpu.VMEM((4, H, SEQ, NOPE), BF16),
            pltpu.SemaphoreType.DMA,
            pltpu.SemaphoreType.DMA((9,)),
            pltpu.SemaphoreType.DMA((9,)),
        ],
        compiler_params=pltpu.CompilerParams(
            collective_id=0, has_side_effects=True, vmem_limit_bytes=VMEM_LIMIT
        ),
        name="spread_queries",
    )(q_nope, w_uk, w_uv)


def attention_kernel(len_ref, q_ref, new_ref, kt_ref, out_ref, top, total, mix):
    b, k = pl.program_id(0), pl.program_id(1)
    length = len_ref[b]

    @pl.when(k == 0)
    def _():
        new = new_ref[0].astype(F32)
        own = jnp.sum(q_ref[0].astype(F32) * new, axis=1, keepdims=True) * SCALE
        top[...] = own
        total[...] = jnp.ones_like(own)
        mix[...] = jnp.broadcast_to(new[:, :KV_RANK], (H, KV_RANK))

    @pl.when(k * BLOCK < length)
    def _():
        s = jnp.dot(q_ref[0], kt_ref[0], preferred_element_type=F32) * SCALE
        pos = lax.broadcasted_iota(jnp.int32, s.shape, 1) + k * BLOCK
        s = jnp.where(pos < length, s, -jnp.inf)
        high = jnp.maximum(top[...], jnp.max(s, axis=1, keepdims=True))
        p = jnp.exp(s - high)
        fade = jnp.exp(top[...] - high)
        total[...] = total[...] * fade + jnp.sum(p, axis=1, keepdims=True)
        top[...] = high
        mix[...] = mix[...] * fade + lax.dot_general(
            p.astype(BF16), kt_ref[0, :KV_RANK, :], NT, preferred_element_type=F32
        )

    @pl.when(k == CACHE // BLOCK - 1)
    def _():
        out_ref[0] = (mix[...] / total[...]).astype(BF16)


def attend(lengths, queries, new_kv, cache_t):
    width = KV_RANK + ROPE
    return pl.pallas_call(
        attention_kernel,
        out_shape=jax.ShapeDtypeStruct((SEQ, H, KV_RANK), BF16),
        grid_spec=pltpu.PrefetchScalarGridSpec(
            num_scalar_prefetch=1,
            grid=(SEQ, CACHE // BLOCK),
            in_specs=[
                pl.BlockSpec((1, H, width), lambda b, k, n: (b, 0, 0)),
                pl.BlockSpec((1, 1, width), lambda b, k, n: (b, 0, 0)),
                pl.BlockSpec(
                    (1, width, BLOCK),
                    lambda b, k, n: (b, 0, jnp.minimum(k, (n[b] - 1) // BLOCK)),
                ),
            ],
            out_specs=pl.BlockSpec((1, H, KV_RANK), lambda b, k, n: (b, 0, 0)),
            scratch_shapes=[
                pltpu.VMEM((H, 1), F32),
                pltpu.VMEM((H, 1), F32),
                pltpu.VMEM((H, KV_RANK), F32),
            ],
        ),
        compiler_params=pltpu.CompilerParams(vmem_limit_bytes=VMEM_LIMIT),
        name="attend",
    )(lengths, queries, new_kv, cache_t)


HALF = D // 2
HALF_CUT = ((0, HALF // 2), (HALF // 2, HALF // 2))


def iota(shape, dim):
    return lax.broadcasted_iota(jnp.int32, shape, dim)


def project_kernel(
    lat_ref, wuv_ref, wout_ref, hidden_ref, gain_ref, wg_ref, wu_ref, wd_ref,
    resid_ref, normed_ref, others_ref,
    got, part_a, part_b, next_a, next_b, last_a, last_b,
    land_a1, land_b1, land_a2, land_b2, pass_a1, pass_b1, pass_a2, pass_b2, land_a3, land_b3,
    send_sems, recv_sems,
):
    at = coordinates()
    r, g, x, z = at["r"], at["g"], at["x"], at["z"]
    y_lo = g // 16
    peers = [(r, (g + k) % 32) for k in range(1, 32)]
    twin = (r + 1 - 2 * at["core"], g)
    barrier_with(peers + [twin])
    copies = Copies(send_sems, recv_sems)
    incoming = [copies.start(lat_ref.at[peer[1]], got.at[g], peer) for peer in peers]
    traded = [
        copies.start(ref, others_ref.at[i], twin) for i, ref in enumerate((wg_ref, wu_ref, wd_ref))
    ]
    got[g] = lat_ref[g]
    for copy in incoming:
        copy.wait_recv()

    heads = jnp.dot(got[...].reshape(256, KV_RANK), wuv_ref[...], preferred_element_type=F32)
    row, col = iota((256, 256), 0), iota((256, 256), 1)
    heads = jnp.where((row & 1) == (col >> 7), heads, 0.0).astype(BF16)
    row, col = iota((128, 256), 0), iota((128, 256), 1)
    b, y_of, low, high = row & 3, (row >> 2) & 1, (row >> 3) & 3, row >> 5

    def project(x_of, z_of, part, first_col):
        source = (((y_of * 4 + x_of) * 4) + z_of) * 4 + b
        pick = jnp.where((col >> 1) == source, 1.0, 0.0).astype(BF16)
        rows = jnp.dot(pick, heads, preferred_element_type=F32).astype(BF16)
        step = HALF // 4
        for n in range(4):
            out = jnp.dot(
                rows, wout_ref[:, pl.ds(first_col + n * step, step)], preferred_element_type=F32
            )
            part[:, :, pl.ds(n * step, step)] = out.astype(BF16).reshape(4, 32, step)

    def ring(axis, src, landing, passing):
        m = at[axis]
        left = device_at(at, **{axis: (m + 3) % 4})
        right = device_at(at, **{axis: (m + 1) % 4})
        return ScatterRing(copies, src, landing, passing, m, left, right, HALF_CUT)

    project(high, low, part_a, 0)
    a1 = ring("x", part_a, land_a1, pass_a1)
    a1.start()
    project(low, high, part_b, HALF)
    b1 = ring("z", part_b, land_b1, pass_b1)
    b1.start()
    a1.middle()
    b1.middle()

    def hand_on(values, ref, count):
        rows = values[0].shape[0] // count
        for (start, size), value in zip(HALF_CUT, values):
            for j in range(count):
                ref[j, :, pl.ds(start, size)] = value[j * rows : (j + 1) * rows].astype(BF16)

    hand_on(a1.end(), next_a, 4)
    a2 = ring("z", next_a, land_a2, pass_a2)
    a2.start()
    hand_on(b1.end(), next_b, 4)
    b2 = ring("x", next_b, land_b2, pass_b2)
    b2.start()
    a2.middle()
    b2.middle()
    across = (r, (g + 16) % 32)
    hand_on(a2.end(), last_a, 2)
    a3 = copies.start(last_a.at[1 - y_lo], land_a3, across)
    hand_on(b2.end(), last_b, 2)
    b3 = copies.start(last_b.at[1 - y_lo], land_b3, across)
    squares = jnp.zeros((SEQ, 1), F32)
    kept = []
    for i, (copy, last, landing) in enumerate(((a3, last_a, land_a3), (b3, last_b, land_b3))):
        copy.wait_recv()
        cols = pl.ds(i * HALF, HALF)
        total = last[y_lo].astype(F32) + landing[...].astype(F32) + hidden_ref[:, cols].astype(F32)
        resid = total.astype(BF16)
        resid_ref[:, cols] = resid
        resid = resid.astype(F32)
        kept.append(resid)
        squares += jnp.sum(resid * resid, axis=1, keepdims=True)
    factor = lax.rsqrt(squares / D + EPS)
    for i in range(2):
        cols = pl.ds(i * HALF, HALF)
        normed_ref[:, cols] = (kept[i] * factor * gain_ref[:, cols].astype(F32)).astype(BF16)
    for copy in traded:
        copy.wait_recv()
    copies.finish()


def project_heads(lat, wuv, w_out, hidden_in, gain, wg_t, wu_t, wd):
    vmem = pl.BlockSpec(memory_space=pltpu.VMEM)
    hbm = pl.BlockSpec(memory_space=pl.ANY)
    count = 31 + 3 + 2 * 13
    half = HALF // 2
    return pl.pallas_call(
        project_kernel,
        out_shape=(
            jax.ShapeDtypeStruct((SEQ, D), BF16),
            jax.ShapeDtypeStruct((SEQ, D), BF16),
            jax.ShapeDtypeStruct((3, FF_OWN, D), BF16),
        ),
        in_specs=[vmem] * 5 + [hbm] * 3,
        out_specs=(vmem, vmem, hbm),
        scratch_shapes=[pltpu.VMEM((32, 8, KV_RANK), BF16)]
        + [pltpu.VMEM((4, 32, HALF), BF16)] * 2
        + [pltpu.VMEM((4, 8, HALF), BF16)] * 2
        + [pltpu.VMEM((2, 4, HALF), BF16)] * 2
        + [pltpu.VMEM((6, 32, half), BF16)] * 2
        + [pltpu.VMEM((6, 8, half), BF16)] * 2
        + [pltpu.VMEM((2, 32, half), BF16)] * 2
        + [pltpu.VMEM((2, 8, half), BF16)] * 2
        + [pltpu.VMEM((4, HALF), BF16)] * 2
        + [pltpu.SemaphoreType.DMA((count,)), pltpu.SemaphoreType.DMA((count,))],
        compiler_params=pltpu.CompilerParams(
            collective_id=1, has_side_effects=True, vmem_limit_bytes=VMEM_LIMIT
        ),
        name="project_heads",
    )(lat, wuv, w_out, hidden_in, gain, wg_t, wu_t, wd)


WIDTHS = (2432, 2432, 2304)
STARTS = (0, 2432, 4864)
CUTS = tuple(
    ((0, (w // 256) * 128 + (w % 256)), ((w // 256) * 128 + (w % 256), (w // 256) * 128)) for w in WIDTHS
)
AXES = (("x", "y", "z"), ("y", "z", "x"), ("z", "x", "y"))


def mlp_kernel(
    normed_ref, resid_ref, wg_ref, wu_ref, wd_ref, others_ref, out_ref,
    gates, downs, sums, turned, *rest,
):
    rest = list(rest)

    def take(n):
        taken, rest[:n] = rest[:n], []
        return taken

    slots, blocks, all_rows = take(3), take(3), take(3)
    parts, nexts, lasts = take(3), take(3), take(3)
    landings = [take(3) for _ in range(3)]
    passings = [take(3) for _ in range(3)]
    local_sems, send_sems, recv_sems = take(3)

    at = coordinates()
    peers = []
    for axis in "xyz":
        for step in (1, 3):
            peers.append(device_at(at, **{axis: (at[axis] + step) % 4}))
    loads = []
    for i, (src, dst) in enumerate(
        (
            (wg_ref, gates.at[0]),
            (others_ref.at[0], gates.at[1]),
            (wu_ref, gates.at[2]),
            (others_ref.at[1], gates.at[3]),
            (wd_ref, downs.at[0]),
            (others_ref.at[2], downs.at[1]),
        )
    ):
        loads.append(pltpu.make_async_copy(src, dst, local_sems.at[i]))
        loads[-1].start()
    barrier_with(peers)
    copies = Copies(send_sems, recv_sems)

    def sides(axis):
        m = at[axis]
        return m, device_at(at, **{axis: (m + 3) % 4}), device_at(at, **{axis: (m + 1) % 4})

    def run(rings):
        for ring in rings:
            ring.start()
        for ring in rings:
            ring.middle()

    def gather(p, axis, block):
        return GatherRing(copies, block, *sides(axis), CUTS[p])

    rings = []
    for p in range(3):
        a, b, c = AXES[p]
        slots[p][at[c]] = normed_ref[:, pl.ds(STARTS[p], WIDTHS[p])]
        ref = slots[p]
        rings.append(gather(p, c, lambda j, cut, ref=ref: ref.at[j, :, pl.ds(*cut)]))
    run(rings)
    later = []
    for p in range(3):
        a, b, c = AXES[p]
        rings[p].end()
        for s in range(4):
            blocks[p][pl.ds(4 * s, 4), :] = slots[p][s].astype(F32)
        all_rows[p][at[a], at[b]] = blocks[p][...].astype(BF16)
        ref = all_rows[p].at[at[a]]
        later.append(gather(p, b, lambda j, cut, ref=ref: ref.at[j, :, pl.ds(*cut)]))
        later[p].start()
    rings = later
    for ring in rings:
        ring.middle()
    later = []
    for p in range(3):
        rings[p].end()
        ref = all_rows[p]
        later.append(gather(p, AXES[p][0], lambda j, cut, ref=ref: ref.at[j, :, :, pl.ds(*cut)]))
        later[p].start()
    for ring in later:
        ring.middle()

    row, col = iota((256, 256), 0), iota((256, 256), 1)

    def place(p, i):
        b = i & 3
        of = {"z": (i >> 2) & 3, "y": (i >> 4) & 3, "x": (i >> 6) & 3}
        s, t, u = (of[axis] for axis in AXES[p])
        return ((s * 4 + t) * 4 + u) * 4 + b

    for load in loads[:4]:
        load.wait()
    for p in range(3):
        later[p].end()
        rows = all_rows[p][...].reshape(256, WIDTHS[p])
        if p > 0:
            order = jnp.where(col == place(p, row), 1.0, 0.0).astype(BF16)
            rows = jnp.dot(order, rows, preferred_element_type=F32).astype(BF16)
        weights = gates[:, :, pl.ds(STARTS[p], WIDTHS[p])].reshape(4 * FF_OWN, WIDTHS[p])
        product = lax.dot_general(weights, rows, NT, preferred_element_type=F32)
        if p > 0:
            product += sums[...]
        sums[...] = product
    gate, up = sums[pl.ds(0, 2 * FF_OWN), :], sums[pl.ds(2 * FF_OWN, 2 * FF_OWN), :]
    turned[...] = (gate / (1.0 + jnp.exp(-gate)) * up).astype(BF16)

    for load in loads[4:]:
        load.wait()

    def scatter(p, axis, phase, src):
        return ScatterRing(copies, src, landings[phase][p], passings[phase][p], *sides(axis), CUTS[p])

    rings = []
    for p in range(3):
        order = jnp.where(row == place(p, col), 1.0, 0.0).astype(BF16)
        act = lax.dot_general(order, turned[...], NT, preferred_element_type=F32).astype(BF16)
        for start, size in CUTS[p]:
            weights = downs[:, :, pl.ds(STARTS[p] + start, size)].reshape(2 * FF_OWN, size)
            out = jnp.dot(act, weights, preferred_element_type=F32)
            parts[p][:, :, pl.ds(start, size)] = out.astype(BF16).reshape(4, 64, size)
        rings.append(scatter(p, AXES[p][0], 0, parts[p]))
        rings[p].start()
    for ring in rings:
        ring.middle()

    def hand_on(p, values, ref):
        rows = values[0].shape[0] // 4
        for (start, size), value in zip(CUTS[p], values):
            for j in range(4):
                ref[j, :, pl.ds(start, size)] = value[j * rows : (j + 1) * rows].astype(BF16)

    for phase, targets in ((1, nexts), (2, lasts)):
        later = []
        for p in range(3):
            hand_on(p, rings[p].end(), targets[p])
            later.append(scatter(p, AXES[p][phase], phase, targets[p]))
            later[p].start()
        rings = later
        for ring in rings:
            ring.middle()
    for p in range(3):
        for (start, size), value in zip(CUTS[p], rings[p].end()):
            cols = pl.ds(STARTS[p] + start, size)
            out_ref[:, cols] = (value + resid_ref[:, cols].astype(F32)).astype(BF16)
    copies.finish()


def mlp(normed, resid, wg_t, wu_t, wd, others):
    vmem = pl.BlockSpec(memory_space=pltpu.VMEM)
    hbm = pl.BlockSpec(memory_space=pl.ANY)
    halves = [cut[0][1] for cut in CUTS]
    scratch = [
        pltpu.VMEM((4, FF_OWN, D), BF16),
        pltpu.VMEM((2, FF_OWN, D), BF16),
        pltpu.VMEM((4 * FF_OWN, 256), F32),
        pltpu.VMEM((2 * FF_OWN, 256), BF16),
    ]
    scratch += [pltpu.VMEM((4, 4, w), BF16) for w in WIDTHS]
    scratch += [pltpu.VMEM((16, w), F32) for w in WIDTHS]
    scratch += [pltpu.VMEM((4, 4, 16, w), BF16) for w in WIDTHS]
    for rows in (64, 16, 4):
        scratch += [pltpu.VMEM((4, rows, w), BF16) for w in WIDTHS]
    for rows in (64, 16, 4):
        scratch += [pltpu.VMEM((6, rows, h), BF16) for h in halves]
    for rows in (64, 16, 4):
        scratch += [pltpu.VMEM((2, rows, h), BF16) for h in halves]
    count = 2 * 3 * 3 * 6
    scratch += [pltpu.SemaphoreType.DMA((n,)) for n in (6, count, count)]
    return pl.pallas_call(
        mlp_kernel,
        out_shape=jax.ShapeDtypeStruct((SEQ, D), BF16),
        in_specs=[vmem] * 2 + [hbm] * 4,
        out_specs=vmem,
        scratch_shapes=scratch,
        compiler_params=pltpu.CompilerParams(
            collective_id=2, has_side_effects=True, vmem_limit_bytes=VMEM_LIMIT
        ),
        name="mlp",
    )(normed, resid, wg_t, wu_t, wd, others)


def on_device(
    hidden_in, q_nope, q_rope, new_kv, cache_kv, lengths,
    w_uk, w_uv, w_out, norm_gain, w_gate, w_up, w_down,
):
    q_lat, value_up = spread_queries(q_nope, w_uk, w_uv)
    q_lat = jnp.transpose(q_lat, (2, 1, 0, 3)).reshape(SEQ, H, KV_RANK)
    queries = jnp.concatenate([q_lat, q_rope.reshape(SEQ, H, ROPE)], axis=2)
    latent = attend(lengths, queries, new_kv[:, None, :], jnp.swapaxes(cache_kv, 1, 2))
    latent = jnp.transpose(latent.reshape(SEQ, 32, 2, KV_RANK), (1, 0, 2, 3)).reshape(32, 8, KV_RANK)
    wg_t, wu_t = w_gate.T, w_up.T
    resid, normed, others = project_heads(
        latent, value_up.reshape(KV_RANK, 256), w_out, hidden_in, norm_gain[None, :], wg_t, wu_t, w_down
    )
    return mlp(normed, resid, wg_t, wu_t, w_down, others)


def solution(mesh):
    return jax.shard_map(
        on_device,
        mesh=mesh,
        in_specs=(
            P(("rep", "grp"), None),
            P(("rep", "grp"), None),
            P(("rep", "grp"), None),
            P(("rep", "grp"), None),
            P(("rep", "grp"), None, None),
            P(("rep", "grp")),
            P("rep", None),
            P("rep", None),
            P("grp", None),
            P(),
            P(None, ("rep", "grp")),
            P(None, ("rep", "grp")),
            P(("rep", "grp"), None),
        ),
        out_specs=P(("rep", "grp"), None),
        check_vma=False,
    )
```

time: 767 us -> 147 us (0.19)
  waiting for transfers between devices: 663 us -> 0 us
  Pallas kernels: 0 us -> 138 us
  matrix products: 48.1 us -> 0 us
  other arithmetic: 15.2 us -> 0.75 us
  between operations: 13.3 us -> 0.05 us
  local copies, waits for them, and re-layouts: 18.3 us -> 8.25 us
  starting transfers between devices: 7.71 us -> 0 us
    psum x1 -> x0, waiting for transfers between devices: 310 us -> none  [on_device(): summed = lax.psum(partial_value.astype(jnp.bfloat16), 'grp')]
    unnamed x5 -> x0, waiting for transfers between devices: 174 us -> none
    all_gather x2 -> x0, waiting for transfers between devices: 170 us -> none  [the longest x1 114 us: in_one_piece(): lax.all_gather(both, axis, axis=dim, tiled=True)]
    pallas_call x0 -> x4, Pallas kernels: none -> 138 us  [the longest x1 61 us: mlp(): pl.pallas_call(mlp_kernel, out_shape=jax.ShapeDtypeStruct((SEQ, D), BF16)...]
    dot_general x8 -> x0, matrix products: 48.1 us -> none  [the longest x1 13.5 us: on_device(): jnp.dot(activated, w_down, preferred_element_type=jnp.float32)]
    split x1 -> x0, local copies, waits for them, and re-layouts: 9.07 us -> none  [in_one_piece(): jnp.split(lax.all_gather(both, axis, axis=dim, tiled=True), ends, axis=al...]
    all_to_all x1 -> x0, waiting for transfers between devices: 8.28 us -> none  [on_device(): lax.all_to_all(head_out, 'grp', split_axis=1, concat_axis=0, tiled=True)]
  transfers between devices with their start and end apart: 5 -> 0, of which waited for: 5 -> 0; matrix products, arithmetic and copies ran while one was open for 0% -> 0% of each run, Pallas kernels for 0% -> 0%
where the time goes in v1:
time: 147 us
  Pallas kernels  138 us (94%)
  local copies, waits for them, and re-layouts  8.25 us (6%)
    pallas_call x1, Pallas kernels, mlp(): pl.pallas_call(mlp_kernel, out_shape=jax.ShapeDtypeStruct((SEQ, D), BF16)...  61 us
    pallas_call x1, Pallas kernels, project_heads(): pl.pallas_call(project_kernel, out_shape=(jax.ShapeDtypeStruct((SEQ, D),...  41.9 us
    pallas_call x1, Pallas kernels, spread_queries(): pl.pallas_call(query_kernel, out_shape=(jax.ShapeDtypeStruct((4, H, SEQ,...  18.1 us
    pallas_call x1, Pallas kernels, attend(): pl.pallas_call(attention_kernel, out_shape=jax.ShapeDtypeStruct((SEQ, H,...  16.7 us

profile of v1, /device:TPU:0, one launch (start us, length us, event | category | flops | bytes accessed | tf_op | source)
XLA Modules:
  0.0 146.8 jit_solution(4063880650938365654)
XLA Ops:
  0.0 1.3 copy.17.new_ref
  1.3 1.3 broadcast_in_dim.7.gain_ref
  2.6 0.9 reshape.16
  3.5 18.1 %spread_queries.1 = (bf16[4,64,4,128]{3,2,1,0:T(4,128)(2,1)}, bf16[4,128,256]{2,1,0:T(8,128)(2,1)}) custom-call(bf16[4,8192]{1,0:T(4,128)(2,1)} %q_ref.1, bf16[128,8192]{1,0:T(8,128)(2,1)} %wuk_ref.1, bf16[128,8192]{1,0:T(8,128)(2,1)} %wuv_ref.1), custom_call_target="tpu_custom_call" | custom-call | tf_op jit(solution)/shard_map/spread_queries/pallas_call | solution.py:182
  21.6 1.2 copy.16
  22.8 0.1 reshape.15
  22.9 0.8 pad_maximum_fusion.q_ref
  23.7 16.7 %attend.1 = bf16[4,64,512]{2,1,0:T(8,128)(2,1)} custom-call(s32[4]{0:T(128)} %len_ref.1, bf16[4,64,576]{2,1,0:T(8,128)(2,1)} %pad_maximum_fusion.q_ref, bf16[4,1,576]{2,1,0:T(2,128)(2,1)} %copy.17.new_ref, bf16[4,576,4096]{2,1,0:T(8,128)(2,1)} %bitcast.9), custom_call_target="tpu_custom_call" | custom-call | tf_op jit(solution)/shard_map/attend/pallas_call | solution.py:245
  40.4 1.1 reshape.17
  41.4 0.2 copy.20
  41.6 0.8 reshape.18.lat_ref
  42.4 41.9 %project_heads.1 = (bf16[4,7168]{1,0:T(4,128)(2,1)}, bf16[4,7168]{1,0:T(4,128)(2,1)}, bf16[3,144,7168]{2,1,0:T(8,128)(2,1)}) custom-call(bf16[32,8,512]{2,1,0:T(8,128)(2,1)} %reshape.18.lat_ref, bf16[512,256]{1,0:T(8,128)(2,1)} %bitcast.15, bf16[256,7168]{1,0:T(8,128)(2,1)} %wout_ref.1, bf16[4,7168]{1,0:T(4,128)(2,1)} %hidden_ref.1, ...), custom_call_target="tpu_custom_call" | custom-call | tf_op jit(solution)/shard_map/project_heads/pallas_call | solution.py:377
  84.4 61.0 %mlp.1 = bf16[4,7168]{1,0:T(4,128)(2,1)} custom-call(bf16[4,7168]{1,0:T(4,128)(2,1)} %get-tuple-element.12.normed_ref, bf16[4,7168]{1,0:T(4,128)(2,1)} %get-tuple-element.13.resid_ref, bf16[144,7168]{1,0:T(8,128)(2,1)} %bitcast.11, bf16[144,7168]{1,0:T(8,128)(2,1)} %bitcast.13, bf16[144,7168]{1,0:T(8,128)(2,1)} %wd_ref.3, ...), custom_call_target="tpu_custom_call" | custom-call | tf_op jit(solution)/shard_map/mlp/pallas_call | solution.py:576
  145.4 1.5 copy.22

commit v2 on v0

v2 whole, which is shorter than its diff:
```python
import functools

import jax
import jax.numpy as jnp
from jax import lax
from jax.experimental import pallas as pl
from jax.experimental.pallas import tpu as pltpu
from jax.sharding import PartitionSpec as P

D = 7168
FF_OWN = 144
H = 64
NOPE = 128
ROPE = 64
VH = 128
KV_RANK = 512
CACHE = 4096
SEQ = 4
BLOCK = 1024
EPS = 1e-06
SCALE = float(NOPE + ROPE) ** (-0.5)
MESH = pl.DeviceIdType.MESH
F32 = jnp.float32
BF16 = jnp.bfloat16
NT = (((1,), (1,)), ((), ()))
VMEM_LIMIT = 62 * 1024 * 1024


def coordinates():
    r, g = lax.axis_index("rep"), lax.axis_index("grp")
    return dict(
        r=r, g=g, core=r % 2, y=(r // 2) * 2 + g // 16, x=(g // 4) % 4, z=g % 4
    )


def device_at(at, **moved):
    x, y, z = (moved.get(k, at[k]) for k in "xyz")
    return ((y // 2) * 2 + at["core"], ((y % 2) * 4 + x) * 4 + z)


class Copies:
    def __init__(self, send_sems, recv_sems):
        self.send, self.recv, self.used, self.all = send_sems, recv_sems, 0, []

    def start(self, src, dst, device):
        k = self.used
        self.used += 1
        copy = pltpu.make_async_remote_copy(
            src_ref=src,
            dst_ref=dst,
            send_sem=self.send.at[k],
            recv_sem=self.recv.at[k],
            device_id=device,
            device_id_type=MESH,
        )
        copy.start()
        self.all.append(copy)
        return copy

    def finish(self):
        for copy in self.all:
            copy.wait_send()


def barrier_with(peers):
    sem = pltpu.get_barrier_semaphore()
    for peer in peers:
        pl.semaphore_signal(sem, inc=1, device_id=peer, device_id_type=MESH)
    pl.semaphore_wait(sem, len(peers))


class GatherRing:
    def __init__(self, copies, block, side, cut):
        self.copies, self.block, self.cut = copies, block, cut
        self.me, self.left, self.right = side

    def go(self, j, half, device):
        ref = self.block(j, self.cut[half])
        return self.copies.start(ref, ref, device)

    def start(self):
        m = self.me
        self.ra = self.go(m, 0, self.right)
        self.lb = self.go(m, 1, self.left)
        self.rb = self.go(m, 1, self.right)
        self.la = self.go(m, 0, self.left)

    def middle(self):
        m = self.me
        self.ra.wait_recv()
        self.rf = self.go((m + 3) % 4, 0, self.right)
        self.lb.wait_recv()
        self.lf = self.go((m + 1) % 4, 1, self.left)

    def near(self):
        self.rb.wait_recv()
        self.la.wait_recv()

    def far(self):
        self.rf.wait_recv()
        self.lf.wait_recv()


class ScatterRing:
    def __init__(self, copies, chunk, landing, passing, side, cut):
        self.copies, self.chunk, self.landing, self.passing, self.cut = copies, chunk, landing, passing, cut
        self.me, self.left, self.right = side

    def part(self, step, half):
        return self.chunk((self.me + step) % 4, self.cut[half])

    def land(self, k, half):
        return self.landing.at[k, :, pl.ds(0, self.cut[half][1])]

    def send_far(self):
        go = self.copies.start
        self.r0 = go(self.part(2, 0), self.land(0, 0), self.right)
        self.l0 = go(self.part(2, 1), self.land(1, 1), self.left)

    def send_right(self):
        self.r1 = self.copies.start(self.part(1, 1), self.land(2, 1), self.right)

    def send_left(self):
        self.l1 = self.copies.start(self.part(3, 0), self.land(3, 0), self.left)

    def start(self):
        self.send_far()
        self.send_right()
        self.send_left()

    def value(self, ref):
        return ref[...].astype(F32)

    def pass_on(self, copy, step, half, device):
        copy.wait_recv()
        held = self.passing.at[half, :, pl.ds(0, self.cut[half][1])]
        held[...] = (self.value(self.part(step, half)) + self.value(self.land(half, half))).astype(BF16)
        return self.copies.start(held, self.land(4 + half, half), device)

    def middle(self):
        self.r2 = self.pass_on(self.r0, 1, 0, self.right)
        self.l2 = self.pass_on(self.l0, 3, 1, self.left)

    def end(self):
        self.l1.wait_recv()
        self.r2.wait_recv()
        first = self.value(self.part(0, 0)) + self.value(self.land(4, 0)) + self.value(self.land(3, 0))
        self.r1.wait_recv()
        self.l2.wait_recv()
        second = self.value(self.part(0, 1)) + self.value(self.land(2, 1)) + self.value(self.land(5, 1))
        return first, second


GROUP = 16


def query_kernel(
    q_ref, rope_ref, wuk_hbm, wuv_ref, out_ref, wuv_out,
    gathered, rows, wuk, tall, made, own_sem, load_sems, send_sems, recv_sems,
):
    at = coordinates()
    r, g = at["r"], at["g"]
    wide = GROUP * NOPE
    spans = [pl.ds(i * wide, wide) for i in range(H // GROUP)]
    loads = [
        pltpu.make_async_copy(wuk_hbm.at[:, span], wuk.at[:, span], load_sems.at[i])
        for i, span in enumerate(spans)
    ]
    for load in loads:
        load.start()
    mine = wuv_ref.at[:, pl.ds(pl.multiple_of(g * 256, 256), 256)]
    own = pltpu.make_async_copy(mine, wuv_out.at[r], own_sem)
    own.start()
    peers = [((r + k) % 4, g) for k in (1, 2, 3)]
    barrier_with(peers)
    copies = Copies(send_sems, recv_sems)
    incoming = [
        [copies.start(q_ref.at[:, span], gathered.at[r, :, span], peer) for peer in peers] for span in spans
    ]
    gathered[r] = q_ref[...]
    out_ref[:, :, pl.ds(KV_RANK, ROPE)] = rope_ref[...]
    slice_of_rank = pl.ds(pl.multiple_of(r * NOPE, NOPE), NOPE)
    back = []
    for i, span in enumerate(spans):
        for copy in incoming[i]:
            copy.wait_recv()
        loads[i].wait()
        for s in range(4):
            rows[pl.ds(4 * s, 4), :] = gathered[s, :, span].astype(F32)
        for k in range(GROUP):
            lat = lax.dot_general(
                rows[:, pl.ds(k * NOPE, NOPE)].astype(BF16),
                wuk[:, pl.ds((i * GROUP + k) * NOPE, NOPE)],
                NT,
                preferred_element_type=F32,
            )
            tall[:, k, :] = lat
        heads = pl.ds(i * GROUP, GROUP)
        made[:, :, heads, :] = tall[...].astype(BF16).reshape(4, SEQ, GROUP, NOPE)
        for peer in peers:
            back.append(
                copies.start(made.at[peer[0], :, heads, :], out_ref.at[:, heads, slice_of_rank], peer)
            )
    weights = [copies.start(mine, wuv_out.at[r], peer) for peer in peers]
    out_ref[:, :, slice_of_rank] = made[r]
    for copy in back + weights:
        copy.wait_recv()
    own.wait()
    copies.finish()


def spread_queries(q_nope, q_rope, w_uk, w_uv):
    vmem = pl.BlockSpec(memory_space=pltpu.VMEM)
    hbm = pl.BlockSpec(memory_space=pl.ANY)
    count = 3 + 6 * (H // GROUP)
    return pl.pallas_call(
        query_kernel,
        out_shape=(
            jax.ShapeDtypeStruct((SEQ, H, KV_RANK + ROPE), BF16),
            jax.ShapeDtypeStruct((4, 128, 256), BF16),
        ),
        in_specs=[vmem, vmem, hbm, hbm],
        out_specs=(vmem, hbm),
        scratch_shapes=[
            pltpu.VMEM((4, SEQ, H * NOPE), BF16),
            pltpu.VMEM((16, GROUP * NOPE), F32),
            pltpu.VMEM((128, H * NOPE), BF16),
            pltpu.VMEM((16, GROUP, NOPE), F32),
            pltpu.VMEM((4, SEQ, H, NOPE), BF16),
            pltpu.SemaphoreType.DMA,
            pltpu.SemaphoreType.DMA((H // GROUP,)),
            pltpu.SemaphoreType.DMA((count,)),
            pltpu.SemaphoreType.DMA((count,)),
        ],
        compiler_params=pltpu.CompilerParams(
            collective_id=0, has_side_effects=True, vmem_limit_bytes=VMEM_LIMIT
        ),
        name="spread_queries",
    )(q_nope, q_rope, w_uk, w_uv)


def attention_kernel(len_ref, q_ref, new_ref, kt_ref, out_ref, scores, lanes, mixed):
    b = pl.program_id(0)
    length = len_ref[b]
    q = q_ref[0]
    pick = lax.broadcasted_iota(jnp.int32, new_ref.shape, 0) == b
    new = jnp.sum(jnp.where(pick, new_ref[...].astype(F32), 0.0), axis=0, keepdims=True)
    own = jnp.sum(q.astype(F32) * new, axis=1, keepdims=True) * SCALE
    lane = lax.broadcasted_iota(jnp.int32, (H, BLOCK), 1)
    top = jnp.full((H, 128), -jnp.inf, F32)
    for c in range(CACHE // BLOCK):
        cols = pl.ds(c * BLOCK, BLOCK)
        s = jnp.dot(q, kt_ref[0, :, cols], preferred_element_type=F32) * SCALE
        s = jnp.where(lane < length - c * BLOCK, s, -jnp.inf)
        scores[:, cols] = s
        for i in range(BLOCK // 128):
            top = jnp.maximum(top, s[:, i * 128 : (i + 1) * 128])
    top = jnp.maximum(jnp.max(top, axis=1, keepdims=True), own)
    own = jnp.exp(own - top)
    total = jnp.zeros((H, 128), F32)
    mix = own * new[:, :KV_RANK]
    for c in range(CACHE // BLOCK):
        cols = pl.ds(c * BLOCK, BLOCK)
        p = jnp.exp(scores[:, cols] - top)
        for i in range(BLOCK // 128):
            total += p[:, i * 128 : (i + 1) * 128]
        mix += lax.dot_general(
            p.astype(BF16), kt_ref[0, :KV_RANK, cols], NT, preferred_element_type=F32
        )
    mix = mix / (jnp.sum(total, axis=1, keepdims=True) + own)
    for t in range(KV_RANK // 128):
        lanes[t] = mix[:, t * 128 : (t + 1) * 128]
        for h in range(2):
            mixed[t, :, 2 * b + h, :] = lanes[t, pl.ds(h, H // 2, stride=2), :]

    @pl.when(b == SEQ - 1)
    def _():
        for t in range(KV_RANK // 128):
            out_ref[:, :, pl.ds(t * 128, 128)] = mixed[t].astype(BF16)


def attend(lengths, queries, new_kv, cache_t):
    width = KV_RANK + ROPE
    return pl.pallas_call(
        attention_kernel,
        out_shape=jax.ShapeDtypeStruct((H // 2, 2 * SEQ, KV_RANK), BF16),
        grid_spec=pltpu.PrefetchScalarGridSpec(
            num_scalar_prefetch=1,
            grid=(SEQ,),
            in_specs=[
                pl.BlockSpec((1, H, width), lambda b, n: (b, 0, 0)),
                pl.BlockSpec((SEQ, width), lambda b, n: (0, 0)),
                pl.BlockSpec((1, width, CACHE), lambda b, n: (b, 0, 0)),
            ],
            out_specs=pl.BlockSpec((H // 2, 2 * SEQ, KV_RANK), lambda b, n: (0, 0, 0)),
            scratch_shapes=[
                pltpu.VMEM((H, CACHE), F32),
                pltpu.VMEM((KV_RANK // 128, H, 128), F32),
                pltpu.VMEM((KV_RANK // 128, H // 2, 2 * SEQ, 128), F32),
            ],
        ),
        compiler_params=pltpu.CompilerParams(vmem_limit_bytes=VMEM_LIMIT),
        name="attend",
    )(lengths, queries, new_kv, cache_t)


HALF = D // 2
HALF_CUT = ((0, HALF // 2), (HALF // 2, HALF // 2))
WIDTHS = (2432, 2432, 2304)
STARTS = (0, 2432, 4864)
CUTS = tuple(
    ((0, (w // 256) * 128 + (w % 256)), ((w // 256) * 128 + (w % 256), (w // 256) * 128)) for w in WIDTHS
)
AXES = (("x", "y", "z"), ("y", "z", "x"), ("z", "x", "y"))
STEPS = (2, 1, 3, 0)


def iota(shape, dim):
    return lax.broadcasted_iota(jnp.int32, shape, dim)


class Taker:
    def __init__(self, refs):
        self.refs = list(refs)

    def __call__(self, n):
        taken, self.refs = self.refs[:n], self.refs[n:]
        return taken


def layer_kernel(
    lat_ref, wuv_ref, wout_hbm, hidden_ref, gain_ref, wg_ref, wu_ref, wd_ref, out_ref,
    got, wout, gates, downs, sums, turned, resid_ref, *rest,
):
    take = Taker(rest)
    part2, next2, land2, last2, land1, pass1, landy = (take(2) for _ in range(7))
    slots, blocks, all_rows = take(3), take(3), take(3)
    parts, nexts, lasts = take(3), take(3), take(3)
    landings, passings, landings2, passings2, landings3 = (take(3) for _ in range(5))
    local_sems, send_sems, recv_sems = take(3)

    at = coordinates()
    r, g = at["r"], at["g"]
    y_lo = g // 16
    loads = []
    for i, (src, dst) in enumerate(
        ((wout_hbm, wout), (wg_ref, gates.at[0]), (wu_ref, gates.at[2]), (wd_ref, downs.at[0]))
    ):
        loads.append(pltpu.make_async_copy(src, dst, local_sems.at[i]))
        loads[-1].start()

    def peer_along(axis, step):
        return device_at(at, **{axis: (at[axis] + step) % 4})

    def side(axis):
        return at[axis], peer_along(axis, 3), peer_along(axis, 1)

    peers = [(r, (g + k) % 32) for k in range(1, 32)]
    twin = (r + 1 - 2 * at["core"], g)
    other = (r + 2) % 4
    barrier_with(peers + [twin, (other, g), (other, (g + 16) % 32)])
    copies = Copies(send_sems, recv_sems)
    incoming = [copies.start(lat_ref.at[peer[1]], got.at[g], peer) for peer in peers]
    traded = [
        copies.start(src, dst, twin)
        for src, dst in ((wg_ref, gates.at[1]), (wu_ref, gates.at[3]), (wd_ref, downs.at[1]))
    ]
    got[g] = lat_ref[g]
    for copy in incoming:
        copy.wait_recv()

    heads = jnp.dot(got[...].reshape(256, KV_RANK), wuv_ref[...], preferred_element_type=F32)
    row, col = iota((256, 256), 0), iota((256, 256), 1)
    heads = jnp.where((row & 1) == (col >> 7), heads, 0.0).astype(BF16)
    row, col = iota((128, 256), 0), iota((128, 256), 1)
    b, y_of, low, high = row & 3, (row >> 2) & 1, (row >> 3) & 3, row >> 5
    loads[0].wait()

    def project(x_of, z_of, part, first_col):
        source = (((y_of * 4 + x_of) * 4) + z_of) * 4 + b
        pick = jnp.where((col >> 1) == source, 1.0, 0.0).astype(BF16)
        rows = jnp.dot(pick, heads, preferred_element_type=F32).astype(BF16)
        step = HALF // 4
        for n in range(4):
            out = jnp.dot(
                rows, wout[:, pl.ds(first_col + n * step, step)], preferred_element_type=F32
            )
            part[:, :, :, pl.ds(n * step, step)] = out.reshape(4, 4, 8, step).astype(BF16)

    axes2 = (("x", "z"), ("z", "x"))
    rings = [[], []]

    def start2(i, k):
        first, second = axes2[i]
        j = (at[second] + STEPS[k]) % 4
        ring = ScatterRing(
            copies,
            lambda t, cut: part2[i].at[t, j, :, pl.ds(*cut)],
            land1[i].at[k],
            pass1[i].at[k],
            side(first),
            HALF_CUT,
        )
        ring.start()
        rings[i].append(ring)

    arriving = [[], []]

    def end2(i, k):
        second = axes2[i][1]
        j = (at[second] + STEPS[k]) % 4
        for cut, value in zip(HALF_CUT, rings[i][k].end()):
            next2[i][j, :, pl.ds(*cut)] = value.astype(BF16)
        if k < 3:
            arriving[i].append(
                copies.start(next2[i].at[j], land2[i].at[k], peer_along(second, STEPS[k]))
            )

    project(high, low, part2[0], 0)
    start2(0, 0)
    start2(0, 1)
    project(low, high, part2[1], HALF)
    start2(1, 0)
    start2(1, 1)
    for k in range(4):
        for i in range(2):
            rings[i][k].middle()
            if k < 2:
                start2(i, k + 2)
        if k > 0:
            for i in range(2):
                end2(i, k - 1)
    for i in range(2):
        end2(i, 3)
    across = (r, (g + 16) % 32)
    paired = []
    for i in range(2):
        total = next2[i][at[axes2[i][1]]].astype(F32)
        for k in range(3):
            arriving[i][k].wait_recv()
            total += land2[i][k].astype(F32)
        for j in range(2):
            last2[i][j] = total[4 * j : 4 * j + 4].astype(BF16)
        paired.append(copies.start(last2[i].at[1 - y_lo], landy[i], across))
    squares = jnp.zeros((SEQ, 1), F32)
    kept = []
    for i in range(2):
        paired[i].wait_recv()
        cols = pl.ds(i * HALF, HALF)
        total = last2[i][y_lo].astype(F32) + landy[i][...].astype(F32) + hidden_ref[:, cols].astype(F32)
        resid = total.astype(BF16)
        resid_ref[:, cols] = resid
        resid = resid.astype(F32)
        kept.append(resid)
        squares += jnp.sum(resid * resid, axis=1, keepdims=True)
    factor = lax.rsqrt(squares / D + EPS)
    normed = jnp.concatenate(kept, axis=1) * factor * gain_ref[...].astype(F32)
    normed = normed.astype(BF16)

    short = []
    for p in range(3):
        c = AXES[p][2]
        slots[p][at[c]] = normed[:, STARTS[p] : STARTS[p] + WIDTHS[p]]
        block = slots[p].at[at[c]]
        short.append([copies.start(block, block, peer_along(c, step)) for step in (2, 1, 3)])
    second = []
    for p in range(3):
        a, b, c = AXES[p]
        for copy in short[p]:
            copy.wait_recv()
        for s in range(4):
            blocks[p][pl.ds(4 * s, 4), :] = slots[p][s].astype(F32)
        all_rows[p][at[a], at[b]] = blocks[p][...].astype(BF16)
        ref = all_rows[p].at[at[a]]
        second.append(
            GatherRing(copies, lambda j, cut, ref=ref: ref.at[j, :, pl.ds(*cut)], side(b), CUTS[p])
        )
        second[p].start()
    third = [{}, {}, {}]

    def start3(p, step):
        a, b, c = AXES[p]
        j = (at[b] + step) % 4
        ring = GatherRing(
            copies, lambda t, cut: all_rows[p].at[t, j, :, pl.ds(*cut)], side(a), CUTS[p]
        )
        ring.start()
        third[p][step] = ring

    every = range(3)
    for p in every:
        start3(p, 0)
    for p in every:
        second[p].middle()
    for p in every:
        second[p].near()
        start3(p, 3)
        start3(p, 1)
    for p in every:
        third[p][0].middle()
    for p in every:
        second[p].far()
        start3(p, 2)
    for step in (3, 1, 2):
        for p in every:
            third[p][step].middle()

    row, col = iota((256, 256), 0), iota((256, 256), 1)

    def place(p, i):
        b = i & 3
        of = {"z": (i >> 2) & 3, "y": (i >> 4) & 3, "x": (i >> 6) & 3}
        s, t, u = (of[axis] for axis in AXES[p])
        return ((s * 4 + t) * 4 + u) * 4 + b

    for load in loads[1:]:
        load.wait()
    for copy in traded:
        copy.wait_recv()
    for p in every:
        for step in (0, 3, 1, 2):
            third[p][step].near()
            third[p][step].far()
        rows = all_rows[p][...].reshape(256, WIDTHS[p])
        if p > 0:
            order = jnp.where(col == place(p, row), 1.0, 0.0).astype(BF16)
            rows = jnp.dot(order, rows, preferred_element_type=F32).astype(BF16)
        weights = gates[:, :, pl.ds(STARTS[p], WIDTHS[p])].reshape(4 * FF_OWN, WIDTHS[p])
        product = lax.dot_general(weights, rows, NT, preferred_element_type=F32)
        if p > 0:
            product += sums[...]
        sums[...] = product
    gate, up = sums[pl.ds(0, 2 * FF_OWN), :], sums[pl.ds(2 * FF_OWN, 2 * FF_OWN), :]
    turned[...] = (gate / (1.0 + jnp.exp(-gate)) * up).astype(BF16)

    first = [[], [], []]

    def start1(p, k):
        a, b, c = AXES[p]
        j = (at[b] + STEPS[k]) % 4
        ring = ScatterRing(
            copies,
            lambda t, cut: parts[p].at[t, j, :, pl.ds(*cut)],
            landings[p].at[k],
            passings[p].at[k],
            side(a),
            CUTS[p],
        )
        ring.start()
        first[p].append(ring)

    second = [
        ScatterRing(
            copies,
            lambda t, cut, p=p: nexts[p].at[t, :, pl.ds(*cut)],
            landings2[p],
            passings2[p],
            side(AXES[p][1]),
            CUTS[p],
        )
        for p in every
    ]

    def end1(p, k):
        j = (at[AXES[p][1]] + STEPS[k]) % 4
        for cut, value in zip(CUTS[p], first[p][k].end()):
            nexts[p][j, :, pl.ds(*cut)] = value.astype(BF16)
        if k < 3:
            (second[p].send_far, second[p].send_right, second[p].send_left)[k]()

    for p in every:
        order = jnp.where(row == place(p, col), 1.0, 0.0).astype(BF16)
        act = lax.dot_general(order, turned[...], NT, preferred_element_type=F32).astype(BF16)
        for start, size in CUTS[p]:
            weights = downs[:, :, pl.ds(STARTS[p] + start, size)].reshape(2 * FF_OWN, size)
            out = jnp.dot(act, weights, preferred_element_type=F32)
            parts[p][:, :, :, pl.ds(start, size)] = out.astype(BF16).reshape(4, 4, 16, size)
        start1(p, 0)
        start1(p, 1)
    for k in range(4):
        for p in every:
            first[p][k].middle()
            if k < 2:
                start1(p, k + 2)
        if k > 0:
            for p in every:
                end1(p, k - 1)
    for p in every:
        second[p].middle()
    for p in every:
        end1(p, 3)
    short = []
    for p in every:
        for (start, size), value in zip(CUTS[p], second[p].end()):
            for j in range(4):
                lasts[p][j, :, pl.ds(start, size)] = value[4 * j : 4 * j + 4].astype(BF16)
        c = AXES[p][2]
        short.append(
            [
                copies.start(lasts[p].at[(at[c] + step) % 4], landings3[p].at[k], peer_along(c, step))
                for k, step in enumerate((2, 1, 3))
            ]
        )
    for p in every:
        cols = pl.ds(STARTS[p], WIDTHS[p])
        total = resid_ref[:, cols].astype(F32) + lasts[p][at[AXES[p][2]]].astype(F32)
        for k in range(3):
            short[p][k].wait_recv()
            total += landings3[p][k].astype(F32)
        out_ref[:, cols] = total.astype(BF16)
    copies.finish()


def layer_tail(lat, wuv, w_out, hidden_in, gain, wg_t, wu_t, wd):
    vmem = pl.BlockSpec(memory_space=pltpu.VMEM)
    hbm = pl.BlockSpec(memory_space=pl.ANY)
    half = HALF // 2
    halves = [cut[0][1] for cut in CUTS]
    scratch = [
        pltpu.VMEM((32, 8, KV_RANK), BF16),
        pltpu.VMEM((256, D), BF16),
        pltpu.VMEM((4, FF_OWN, D), BF16),
        pltpu.VMEM((2, FF_OWN, D), BF16),
        pltpu.VMEM((4 * FF_OWN, 256), F32),
        pltpu.VMEM((2 * FF_OWN, 256), BF16),
        pltpu.VMEM((SEQ, D), BF16),
    ]
    for shape in (
        (4, 4, 8, HALF), (4, 8, HALF), (3, 8, HALF), (2, 4, HALF), (4, 6, 8, half), (4, 2, 8, half), (4, HALF),
    ):
        scratch += [pltpu.VMEM(shape, BF16)] * 2
    scratch += [pltpu.VMEM((4, 4, w), BF16) for w in WIDTHS]
    scratch += [pltpu.VMEM((16, w), F32) for w in WIDTHS]
    for lead in ((4, 4, 16), (4, 4, 16), (4, 16), (4, 4)):
        scratch += [pltpu.VMEM((*lead, w), BF16) for w in WIDTHS]
    for lead in ((4, 6, 16), (4, 2, 16), (6, 16), (2, 16)):
        scratch += [pltpu.VMEM((*lead, h), BF16) for h in halves]
    scratch += [pltpu.VMEM((3, 4, w), BF16) for w in WIDTHS]
    count = 31 + 3 + 2 * (24 + 3 + 1) + 3 * (3 + 6 + 24) * 2
    scratch += [pltpu.SemaphoreType.DMA((n,)) for n in (4, count, count)]
    return pl.pallas_call(
        layer_kernel,
        out_shape=jax.ShapeDtypeStruct((SEQ, D), BF16),
        in_specs=[vmem] * 2 + [hbm] + [vmem] * 2 + [hbm] * 3,
        out_specs=vmem,
        scratch_shapes=scratch,
        compiler_params=pltpu.CompilerParams(
            collective_id=1, has_side_effects=True, vmem_limit_bytes=VMEM_LIMIT
        ),
        name="layer_tail",
    )(lat, wuv, w_out, hidden_in, gain, wg_t, wu_t, wd)


def on_device(
    hidden_in, q_nope, q_rope, new_kv, cache_kv, lengths,
    w_uk, w_uv, w_out, norm_gain, w_gate, w_up, w_down,
):
    queries, value_up = spread_queries(q_nope, q_rope.reshape(SEQ, H, ROPE), w_uk, w_uv)
    latent = attend(lengths, queries, new_kv, jnp.swapaxes(cache_kv, 1, 2))
    return layer_tail(
        latent, value_up.reshape(KV_RANK, 256), w_out, hidden_in, norm_gain[None, :], w_gate.T, w_up.T, w_down
    )


def solution(mesh):
    return jax.shard_map(
        on_device,
        mesh=mesh,
        in_specs=(
            P(("rep", "grp"), None),
            P(("rep", "grp"), None),
            P(("rep", "grp"), None),
            P(("rep", "grp"), None),
            P(("rep", "grp"), None, None),
            P(("rep", "grp")),
            P("rep", None),
            P("rep", None),
            P("grp", None),
            P(),
            P(None, ("rep", "grp")),
            P(None, ("rep", "grp")),
            P(("rep", "grp"), None),
        ),
        out_specs=P(("rep", "grp"), None),
        check_vma=False,
    )
```

time: 767 us -> 123 us (0.16)
  waiting for transfers between devices: 663 us -> 0 us
  Pallas kernels: 0 us -> 119 us
  matrix products: 48.1 us -> 0 us
  other arithmetic: 15.2 us -> 0 us
  local copies, waits for them, and re-layouts: 18.3 us -> 3.58 us
  between operations: 13.3 us -> 0.03 us
  starting transfers between devices: 7.71 us -> 0 us
    psum x1 -> x0, waiting for transfers between devices: 310 us -> none  [on_device(): summed = lax.psum(partial_value.astype(jnp.bfloat16), 'grp')]
    unnamed x5 -> x0, waiting for transfers between devices: 174 us -> none
    all_gather x2 -> x0, waiting for transfers between devices: 170 us -> none  [the longest x1 114 us: in_one_piece(): lax.all_gather(both, axis, axis=dim, tiled=True)]
    pallas_call x0 -> x3, Pallas kernels: none -> 119 us  [the longest x1 87.5 us: layer_tail(): pl.pallas_call(layer_kernel, out_shape=jax.ShapeDtypeStruct((SEQ, D), BF1...]
    dot_general x8 -> x0, matrix products: 48.1 us -> none  [the longest x1 13.5 us: on_device(): jnp.dot(activated, w_down, preferred_element_type=jnp.float32)]
    split x1 -> x0, local copies, waits for them, and re-layouts: 9.07 us -> none  [in_one_piece(): jnp.split(lax.all_gather(both, axis, axis=dim, tiled=True), ends, axis=al...]
    all_to_all x1 -> x0, waiting for transfers between devices: 8.28 us -> none  [on_device(): lax.all_to_all(head_out, 'grp', split_axis=1, concat_axis=0, tiled=True)]
  transfers between devices with their start and end apart: 5 -> 0, of which waited for: 5 -> 0; matrix products, arithmetic and copies ran while one was open for 0% -> 0% of each run, Pallas kernels for 0% -> 0%
where the time goes in v2:
time: 123 us
  Pallas kernels  119 us (97%)
  local copies, waits for them, and re-layouts  3.58 us (3%)
    pallas_call x1, Pallas kernels, layer_tail(): pl.pallas_call(layer_kernel, out_shape=jax.ShapeDtypeStruct((SEQ, D), BF1...  87.5 us
    pallas_call x1, Pallas kernels, spread_queries(): pl.pallas_call(query_kernel, out_shape=(jax.ShapeDtypeStruct((SEQ, H, KV_...  17.1 us
    pallas_call x1, Pallas kernels, attend(): pl.pallas_call(attention_kernel, out_shape=jax.ShapeDtypeStruct((H // 2,...  14.4 us

profile of v2, /device:TPU:0, one launch (start us, length us, event | category | flops | bytes accessed | tf_op | source)
XLA Modules:
  0.0 122.6 jit_solution(1223227657997337980)
XLA Ops:
  0.0 1.5 %reshape.6.rope_ref = bf16[4,64,64]{2,1,0:T(8,128)(2,1)} reshape(bf16[4,4096]{1,0:T(4,128)(2,1)} %param.15) | data formatting | bytes 65536 | tf_op jit(solution)/shard_map/reshape | solution.py:658
  1.5 17.1 %spread_queries.1 = (bf16[4,64,576]{2,1,0:T(8,128)(2,1)}, bf16[4,128,256]{2,1,0:T(8,128)(2,1)}) custom-call(bf16[4,8192]{1,0:T(4,128)(2,1)} %q_ref.1, bf16[4,64,64]{2,1,0:T(8,128)(2,1)} %reshape.6.rope_ref, bf16[128,8192]{1,0:T(8,128)(2,1)} %wuk_hbm.1, bf16[128,8192]{1,0:T(8,128)(2,1)} %wuv_ref.1), custom_call_target="tpu_custom_call" | custom-call | tf_op jit(solution)/shard_map/spread_queries/pallas_call | solution.py:216
  18.6 0.0 copy-start
  18.6 14.4 %attend.1.lat_ref = bf16[32,8,512]{2,1,0:T(8,128)(2,1)} custom-call(s32[4]{0:T(128)} %len_ref.1, bf16[4,64,576]{2,1,0:T(8,128)(2,1)} %get-tuple-element.7.q_ref, bf16[4,576]{1,0:T(4,128)(2,1)} %new_ref.1, bf16[4,576,4096]{2,1,0:T(8,128)(2,1)} %bitcast.4), custom_call_target="tpu_custom_call" | custom-call | tf_op jit(solution)/shard_map/attend/pallas_call | solution.py:284
  33.0 0.0 copy-done
  33.0 0.6 broadcast_in_dim.3.gain_ref
  33.6 87.5 %layer_tail.1 = bf16[4,7168]{1,0:T(4,128)(2,1)} custom-call(bf16[32,8,512]{2,1,0:T(8,128)(2,1)} %attend.1.lat_ref, bf16[512,256]{1,0:T(8,128)(2,1)} %bitcast.7, bf16[256,7168]{1,0:T(8,128)(2,1)} %wout_hbm.1, bf16[4,7168]{1,0:T(4,128)(2,1)} %hidden_ref.1, bf16[1,7168]{1,0:T(2,128)(2,1)} %broadcast_in_dim.3.gain_ref, bf16[144,7168]{1,0:T(8,128)(2,1)} %bitcast.5, ...), custom_call_target="tpu_custom_call" | custom-call | tf_op jit(solution)/shard_map/layer_tail/pallas_call | solution.py:641
  121.1 1.5 %copy.15 = bf16[4,7168]{1,0:T(4,128)(2,1)} copy(bf16[4,7168]{1,0:T(4,128)(2,1)} %layer_tail.1) | data formatting | bytes 114688
Async XLA Ops:
  18.6 14.4 %copy-start = (bf16[7168]{0:T(1024)(128)(2,1)S(1)}, bf16[7168]{0:T(1024)(128)(2,1)}, u32[]{:S(2)}) copy-start(bf16[7168]{0:T(1024)(128)(2,1)} %param.22) | copy-start | bytes 43012

commit v3 on v0

v3 whole, which is shorter than its diff:
```python
import functools

import jax
import jax.numpy as jnp
from jax import lax
from jax.experimental import pallas as pl
from jax.experimental.pallas import tpu as pltpu
from jax.sharding import PartitionSpec as P

D = 7168
FF_OWN = 144
H = 64
NOPE = 128
ROPE = 64
VH = 128
KV_RANK = 512
CACHE = 4096
SEQ = 4
NB = SEQ
BLOCK = 1024
DIRECT_GATHER = (2,)
DIRECT_SCATTER = (2, 3)
DIRECT_PROJECT = (2, 3)
LAG = 1
RINGS = 4 - len(DIRECT_SCATTER)
RINGS_PROJECT = 4 - len(DIRECT_PROJECT)
START_AHEAD = 2
EPS = 1e-06
SCALE = float(NOPE + ROPE) ** (-0.5)
MESH = pl.DeviceIdType.MESH
F32 = jnp.float32
BF16 = jnp.bfloat16
NT = (((1,), (1,)), ((), ()))
VMEM_LIMIT = 67043328


def coordinates():
    r, g = lax.axis_index("rep"), lax.axis_index("grp")
    return dict(
        r=r, g=g, core=r % 2, y=(r // 2) * 2 + g // 16, x=(g // 4) % 4, z=g % 4
    )


def device_at(at, **moved):
    x, y, z = (moved.get(k, at[k]) for k in "xyz")
    return ((y // 2) * 2 + at["core"], ((y % 2) * 4 + x) * 4 + z)


class Copies:
    def __init__(self, send_sems, recv_sems):
        self.send, self.recv, self.used, self.all = send_sems, recv_sems, 0, []

    def start(self, src, dst, device):
        k = self.used
        self.used += 1
        copy = pltpu.make_async_remote_copy(
            src_ref=src,
            dst_ref=dst,
            send_sem=self.send.at[k],
            recv_sem=self.recv.at[k],
            device_id=device,
            device_id_type=MESH,
        )
        copy.start()
        self.all.append(copy)
        return copy

    def finish(self):
        for copy in self.all:
            copy.wait_send()


def barrier_with(peers):
    sem = pltpu.get_barrier_semaphore()
    for peer in peers:
        pl.semaphore_signal(sem, inc=1, device_id=peer, device_id_type=MESH)
    pl.semaphore_wait(sem, len(peers))


class GatherRing:
    def __init__(self, copies, block, side, cut):
        self.copies, self.block, self.cut = copies, block, cut
        self.me, self.left, self.right = side

    def go(self, j, half, device):
        ref = self.block(j, self.cut[half])
        return self.copies.start(ref, ref, device)

    def start(self):
        m = self.me
        self.ra = self.go(m, 0, self.right)
        self.lb = self.go(m, 1, self.left)
        self.rb = self.go(m, 1, self.right)
        self.la = self.go(m, 0, self.left)

    def middle(self):
        m = self.me
        self.ra.wait_recv()
        self.rf = self.go((m + 3) % 4, 0, self.right)
        self.lb.wait_recv()
        self.lf = self.go((m + 1) % 4, 1, self.left)

    def near(self):
        self.rb.wait_recv()
        self.la.wait_recv()

    def far(self):
        self.rf.wait_recv()
        self.lf.wait_recv()


class ScatterRing:
    def __init__(self, copies, chunk, landing, passing, side, cut):
        self.copies, self.chunk, self.landing, self.passing, self.cut = copies, chunk, landing, passing, cut
        self.me, self.left, self.right = side

    def part(self, step, half):
        return self.chunk((self.me + step) % 4, self.cut[half])

    def land(self, k, half):
        return self.landing.at[k, :, pl.ds(0, self.cut[half][1])]

    def send_far(self):
        go = self.copies.start
        self.r0 = go(self.part(2, 0), self.land(0, 0), self.right)
        self.l0 = go(self.part(2, 1), self.land(1, 1), self.left)

    def send_right(self):
        self.r1 = self.copies.start(self.part(1, 1), self.land(2, 1), self.right)

    def send_left(self):
        self.l1 = self.copies.start(self.part(3, 0), self.land(3, 0), self.left)

    def start(self):
        self.send_far()
        self.send_right()
        self.send_left()

    def value(self, ref):
        return ref[...].astype(F32)

    def pass_on(self, copy, step, half, device):
        copy.wait_recv()
        held = self.passing.at[half, :, pl.ds(0, self.cut[half][1])]
        held[...] = self.part(step, half)[...] + self.land(half, half)[...]
        return self.copies.start(held, self.land(4 + half, half), device)

    def middle(self):
        self.r2 = self.pass_on(self.r0, 1, 0, self.right)
        self.l2 = self.pass_on(self.l0, 3, 1, self.left)

    def end(self):
        self.l1.wait_recv()
        self.r2.wait_recv()
        first = self.value(self.part(0, 0)) + self.value(self.land(4, 0)) + self.value(self.land(3, 0))
        self.r1.wait_recv()
        self.l2.wait_recv()
        second = self.value(self.part(0, 1)) + self.value(self.land(2, 1)) + self.value(self.land(5, 1))
        return first, second


class GatherDirect:
    def __init__(self, copies, block, me, devices):
        self.copies, self.block, self.me, self.devices = copies, block, me, devices

    def start(self):
        ref = self.block(self.me)
        self.sent = [self.copies.start(ref, ref, device) for device in self.devices]

    def middle(self):
        pass

    def near(self):
        pass

    def far(self):
        for copy in self.sent:
            copy.wait_recv()


class ScatterDirect:
    def __init__(self, copies, chunk, landing, me, devices, cut):
        self.copies, self.chunk, self.landing, self.me = copies, chunk, landing, me
        self.devices, self.cut = devices, cut

    def start(self):
        width = sum(size for _, size in self.cut)
        self.sent = [
            self.copies.start(
                self.chunk((self.me + step) % 4, (0, width)), self.landing.at[i, :, pl.ds(0, width)], device
            )
            for i, (step, device) in enumerate(zip((2, 1, 3), self.devices))
        ]

    def middle(self):
        pass

    def end(self):
        for copy in self.sent:
            copy.wait_recv()
        values = []
        for start, size in self.cut:
            value = self.chunk(self.me, (start, size))[...].astype(F32)
            for i in range(3):
                value += self.landing[i, :, pl.ds(start, size)].astype(F32)
            values.append(value)
        return values


GROUP = 16
HALF = D // 2
HALF_CUT = ((0, HALF // 2), (HALF // 2, HALF // 2))
WIDTHS = (2432, 2432, 2304)
STARTS = (0, 2432, 4864)
CUTS = tuple(
    ((0, (w // 256) * 128 + (w % 256)), ((w // 256) * 128 + (w % 256), (w // 256) * 128)) for w in WIDTHS
)
AXES = (("x", "y", "z"), ("y", "z", "x"), ("z", "x", "y"))
AXES2 = (("x", "z"), ("z", "x"))
STEPS = (2, 1, 3, 0)
LB = NB.bit_length() - 1


def iota(shape, dim):
    return lax.broadcasted_iota(jnp.int32, shape, dim)


class Named:
    def __init__(self):
        self.names, self.shapes = [], []

    def add(self, name, *shapes):
        self.names.append((name, len(shapes)))
        self.shapes += shapes

    def bind(self, refs):
        refs = list(refs)
        for name, count in self.names:
            taken, refs = refs[:count], refs[count:]
            setattr(self, name, taken[0] if count == 1 else taken)
        return self


def declare():
    s = Named()
    half = HALF // 2
    halves = [cut[0][1] for cut in CUTS]
    b16 = lambda *shape: pltpu.VMEM(shape, BF16)
    f32 = lambda *shape: pltpu.VMEM(shape, F32)
    s.add("gathered", b16(4, SEQ, H * NOPE))
    s.add("rows", f32(16, GROUP * NOPE))
    s.add("wuk", b16(128, H * NOPE))
    s.add("tall", f32(16, GROUP, NOPE))
    s.add("made", b16(4, SEQ, H, NOPE))
    s.add("queries", b16(SEQ, H, KV_RANK + ROPE))
    s.add("wuv", b16(4, 128, 256))
    s.add("cache", b16(SEQ, KV_RANK + ROPE, CACHE))
    s.add("scores", f32(SEQ, H, CACHE))
    s.add("lanes", f32(KV_RANK // 128, H, 128))
    s.add("mixed", f32(KV_RANK // 128, H // 2, NB, 128))
    s.add("wout", b16(256, D))
    s.add("gates", b16(4, FF_OWN, D))
    s.add("downs", b16(2, FF_OWN, D))
    s.add("sums", f32(4 * FF_OWN, 64 * NB))
    s.add("turned", b16(2 * FF_OWN, 64 * NB))
    s.add("blocks", *[f32(4 * NB, w) for w in WIDTHS])
    s.add("gain", f32(1, D))
    s.add("rope", f32(SEQ, H, 128))
    for f in range(1):
        s.add(f"lat{f}", b16(H // 2, 2, NB, KV_RANK))
        s.add(f"got{f}", b16(H // 2, 2, NB, KV_RANK))
        s.add(f"resid{f}", f32(NB, D))
        for name, shape in (
            ("part2", (4, 4, 2 * NB, HALF)),
            ("next2", (4, 2, NB, HALF)),
            ("land2", (7, NB, HALF)),
            ("land1", (RINGS_PROJECT, 6, 2 * NB, half)),
            ("pass1", (RINGS_PROJECT, 2, 2 * NB, half)),
            ("whole1", (4 - RINGS_PROJECT, 3, 2 * NB, HALF)),
        ):
            s.add(f"{name}{f}", *[b16(*shape)] * 2)
        for name, lead in (
            ("slots", (4, 4, NB)),
            ("all_rows", (4, 4, 4 * NB)),
            ("parts", (4, 4, 4 * NB)),
            ("lasts", (4, 4, NB)),
            ("landings3", (15, NB)),
            ("wholes", (4 - RINGS, 3, 4 * NB)),
        ):
            s.add(f"{name}{f}", *[b16(*lead, w) for w in WIDTHS])
        for name, lead in (
            ("landings", (RINGS, 6, 4 * NB)),
            ("passings", (RINGS, 2, 4 * NB)),
        ):
            s.add(f"{name}{f}", *[b16(*lead, h) for h in halves])
    count = 6 + 6 * (H // GROUP) + 62 + 2 * (24 + 7) + 3 * (15 + 24) * 2
    s.add("local_sems", pltpu.SemaphoreType.DMA((5,)))
    s.add("wuk_sems", pltpu.SemaphoreType.DMA((H // GROUP,)))
    s.add("cache_sems", pltpu.SemaphoreType.DMA((SEQ,)))
    s.add("send_sems", pltpu.SemaphoreType.DMA((count,)))
    s.add("recv_sems", pltpu.SemaphoreType.DMA((count,)))
    return s


def layer_kernel(
    len_ref, q_ref, rope_ref, new_ref, hidden_ref, gain_ref,
    cache_hbm, wuk_hbm, wuv_hbm, wout_hbm, wg_hbm, wu_hbm, wd_hbm, out_ref, *refs,
):
    s = declare().bind(refs)
    at = coordinates()
    r, g = at["r"], at["g"]
    y_lo = g // 16
    copies = Copies(s.send_sems, s.recv_sems)
    every = range(3)

    def peer_along(axis, step):
        return device_at(at, **{axis: (at[axis] + step) % 4})

    def side(axis):
        return at[axis], peer_along(axis, 3), peer_along(axis, 1)

    def three(axis):
        return [peer_along(axis, step) for step in (2, 1, 3)]

    wide = GROUP * NOPE
    spans = [pl.ds(i * wide, wide) for i in range(H // GROUP)]
    wuk_loads = [
        pltpu.make_async_copy(wuk_hbm.at[:, span], s.wuk.at[:, span], s.wuk_sems.at[i])
        for i, span in enumerate(spans)
    ]
    mine = wuv_hbm.at[:, pl.ds(pl.multiple_of(g * 256, 256), 256)]
    own_wuv = pltpu.make_async_copy(mine, s.wuv.at[r], s.local_sems.at[4])
    cache_loads = [
        pltpu.make_async_copy(cache_hbm.at[b], s.cache.at[b], s.cache_sems.at[b]) for b in range(SEQ)
    ]
    loads = [
        pltpu.make_async_copy(src, dst, s.local_sems.at[i])
        for i, (src, dst) in enumerate(
            ((wout_hbm, s.wout), (wg_hbm, s.gates.at[0]), (wu_hbm, s.gates.at[2]), (wd_hbm, s.downs.at[0]))
        )
    ]
    for load in wuk_loads + [own_wuv] + cache_loads + loads:
        load.start()

    twin = (r + 1 - 2 * at["core"], g)
    other = (r + 2) % 4
    cousins = [((r + k) % 4, g) for k in (1, 2, 3)]
    peers = [(r, (g + k) % 32) for k in range(1, 32)]
    across = (r, (g + 16) % 32)
    far_y = [
        device_at(at, **{axis: (at[axis] + k) % 4, "y": 2 * (1 - at["y"] // 2) + j})
        for axis in "xz"
        for k in range(4)
        for j in range(2)
        if axis == "x" or k > 0
    ]
    near_y = [(r + 1 - 2 * at["core"], g), (other + 1 - 2 * at["core"], g)]
    barrier_with(peers + near_y + far_y)

    incoming = [
        [copies.start(q_ref.at[:, span], s.gathered.at[r, :, span], peer) for peer in cousins]
        for span in spans
    ]
    s.gathered[r] = q_ref[...]
    for k in range(H // 2):
        pair = rope_ref[:, pl.ds(k * 128, 128)].astype(F32)
        s.rope[:, 2 * k, :] = pair
        s.rope[:, 2 * k + 1, :] = pltpu.roll(pair, 64, 1)
    s.queries[:, :, pl.ds(KV_RANK, ROPE)] = s.rope[:, :, pl.ds(0, ROPE)].astype(BF16)
    gain = gain_ref[...].astype(F32)
    for k in range(D // 128):
        s.gain[:, pl.ds(k * 128, 128)] = gain[k : k + 1]
    slice_of_rank = pl.ds(pl.multiple_of(r * NOPE, NOPE), NOPE)
    new_rows = new_ref[...].astype(F32)

    def rotary_scores(b):
        length = len_ref[b]
        q = s.rope[b, :, pl.ds(0, ROPE)].astype(BF16)
        lane = iota((H, BLOCK), 1)
        cache_loads[b].wait()
        for c in range(CACHE // BLOCK):
            cols = pl.ds(c * BLOCK, BLOCK)
            v = jnp.dot(q, s.cache[b, pl.ds(KV_RANK, ROPE), cols], preferred_element_type=F32) * SCALE
            s.scores[b, :, cols] = jnp.where(lane < length - c * BLOCK, v, -jnp.inf)

    rotary_scores(0)
    rotary_scores(1)
    back = []
    for i, span in enumerate(spans):
        for copy in incoming[i]:
            copy.wait_recv()
        wuk_loads[i].wait()
        for m in range(4):
            s.rows[pl.ds(4 * m, 4), :] = s.gathered[m, :, span].astype(F32)
        for k in range(GROUP):
            s.tall[:, k, :] = lax.dot_general(
                s.rows[:, pl.ds(k * NOPE, NOPE)].astype(BF16),
                s.wuk[:, pl.ds((i * GROUP + k) * NOPE, NOPE)],
                NT,
                preferred_element_type=F32,
            )
        heads = pl.ds(i * GROUP, GROUP)
        s.made[:, :, heads, :] = s.tall[...].astype(BF16).reshape(4, SEQ, GROUP, NOPE)
        for peer in cousins:
            back.append(
                copies.start(s.made.at[peer[0], :, heads, :], s.queries.at[:, heads, slice_of_rank], peer)
            )
    weights = [copies.start(mine, s.wuv.at[r], peer) for peer in cousins]
    traded = [
        copies.start(src, dst, twin)
        for src, dst in ((wg_hbm, s.gates.at[1]), (wu_hbm, s.gates.at[3]), (wd_hbm, s.downs.at[1]))
    ]
    s.queries[:, :, slice_of_rank] = s.made[r]
    rotary_scores(2)
    rotary_scores(3)
    for copy in back:
        copy.wait_recv()

    def attend(b, local):
        q = s.queries[b]
        new = new_rows[b : b + 1]
        own = jnp.sum(q.astype(F32) * new, axis=1, keepdims=True) * SCALE
        q = q[:, :KV_RANK]
        top = jnp.full((H, 128), -jnp.inf, F32)
        for c in range(CACHE // BLOCK):
            cols = pl.ds(c * BLOCK, BLOCK)
            v = jnp.dot(q, s.cache[b, pl.ds(0, KV_RANK), cols], preferred_element_type=F32) * SCALE
            v += s.scores[b, :, cols]
            s.scores[b, :, cols] = v
            for i in range(BLOCK // 128):
                top = jnp.maximum(top, v[:, i * 128 : (i + 1) * 128])
        top = jnp.maximum(jnp.max(top, axis=1, keepdims=True), own)
        own = jnp.exp(own - top)
        total = jnp.zeros((H, 128), F32)
        mix = own * new[:, :KV_RANK]
        for c in range(CACHE // BLOCK):
            cols = pl.ds(c * BLOCK, BLOCK)
            p = jnp.exp(s.scores[b, :, cols] - top)
            for i in range(BLOCK // 128):
                total += p[:, i * 128 : (i + 1) * 128]
            mix += lax.dot_general(
                p.astype(BF16), s.cache[b, pl.ds(0, KV_RANK), cols], NT, preferred_element_type=F32
            )
        mix = mix / (jnp.sum(total, axis=1, keepdims=True) + own)
        for t in range(KV_RANK // 128):
            s.lanes[t] = mix[:, t * 128 : (t + 1) * 128]
            for h in range(2):
                s.mixed[t, :, 2 * local + h, :] = s.lanes[t, pl.ds(h, H // 2, stride=2), :]

    def place(p, i):
        b = i & (NB - 1)
        of = {"z": (i >> LB) & 3, "y": (i >> (LB + 2)) & 3, "x": (i >> (LB + 4)) & 3}
        t, u, v = (of[axis] for axis in AXES[p])
        return ((t * 4 + u) * 4 + v) * NB + b

    lat, got = s.lat0, s.got0

    def send_latents(pair):
        for t in range(KV_RANK // 128):
            lat[:, pair, :, pl.ds(t * 128, 128)] = s.mixed[t].astype(BF16)
        return [copies.start(lat.at[peer[1], pair], got.at[g, pair], peer) for peer in peers]

    def flow(f):
        buf = lambda name: getattr(s, f"{name}{f}")
        arriving = send_latents(1)
        got[g] = lat[g]
        yield
        for copy in early + arriving:
            copy.wait_recv()
        if f == 0:
            for copy in weights:
                copy.wait_recv()
            own_wuv.wait()
            loads[0].wait()
        rows_in = got[...].reshape(64 * NB, KV_RANK)
        heads = jnp.dot(rows_in, s.wuv[...].reshape(KV_RANK, 256), preferred_element_type=F32)
        row, col = iota((64 * NB, 256), 0), iota((64 * NB, 256), 1)
        heads = jnp.where((row & 1) == (col >> 7), heads, 0.0).astype(BF16)
        row, col = iota((32 * NB, 64 * NB), 0), iota((32 * NB, 64 * NB), 1)
        b, y_of, low, high = row & (NB - 1), (row >> LB) & 1, (row >> (LB + 1)) & 3, row >> (LB + 3)
        part2, next2, land2 = buf("part2"), buf("next2"), buf("land2")
        rings = [[], []]
        gathering = [[], []]

        def project(x_of, z_of, part, first_col):
            source = (((y_of * 4 + x_of) * 4) + z_of) * NB + b
            pick = jnp.where((col >> 1) == source, 1.0, 0.0).astype(BF16)
            rows = jnp.dot(pick, heads, preferred_element_type=F32).astype(BF16)
            step = HALF // 4
            for n in range(4):
                out = jnp.dot(
                    rows, s.wout[:, pl.ds(first_col + n * step, step)], preferred_element_type=F32
                )
                part[:, :, :, pl.ds(n * step, step)] = out.reshape(4, 4, 2 * NB, step).astype(BF16)

        def start2(i, k):
            j = (at[AXES2[i][1]] + STEPS[k]) % 4
            first = AXES2[i][0]
            chunk = lambda t, cut: part2[i].at[t, j, :, pl.ds(*cut)]
            if k in DIRECT_PROJECT:
                ring = ScatterDirect(copies, chunk, buf("whole1")[i].at[k - RINGS_PROJECT], at[first], three(first), HALF_CUT)
            else:
                ring = ScatterRing(
                    copies, chunk, buf("land1")[i].at[k], buf("pass1")[i].at[k], side(first), HALF_CUT
                )
            ring.start()
            rings[i].append(ring)

        def end2(i, k):
            second = AXES2[i][1]
            j = (at[second] + STEPS[k]) % 4
            for cut, value in zip(HALF_CUT, rings[i][k].end()):
                for half in range(2):
                    next2[i][j, half, :, pl.ds(*cut)] = value[NB * half : NB * half + NB].astype(BF16)
            for step in (1, 0):
                if k < 3 or step > 0:
                    to = (y_lo + step) % 2
                    device = device_at(at, **{second: j, "y": at["y"] - y_lo + to})
                    landing = land2[i].at[len(gathering[i])]
                    gathering[i].append(copies.start(next2[i].at[j, to], landing, device))

        project(high, low, part2[0], 0)
        start2(0, 0)
        start2(0, 1)
        project(low, high, part2[1], HALF)
        start2(1, 0)
        start2(1, 1)
        for k in range(4):
            yield
            for i in range(2):
                rings[i][k].middle()
                if k < 2:
                    start2(i, k + 2)
            if k >= LAG:
                for i in range(2):
                    end2(i, k - LAG)
        for k in range(4 - LAG, 4):
            yield
            for i in range(2):
                end2(i, k)
        yield
        squares = jnp.zeros((NB, 1), F32)
        kept = []
        for i in range(2):
            cols = pl.ds(i * HALF, HALF)
            total = next2[i][at[AXES2[i][1]], y_lo].astype(F32) + hidden_ref[:, cols].astype(F32)
            for k in range(7):
                gathering[i][k].wait_recv()
                total += land2[i][k].astype(F32)
            resid = total.astype(BF16).astype(F32)
            buf("resid")[:, cols] = resid
            kept.append(resid)
            squares += jnp.sum(resid * resid, axis=1, keepdims=True)
        factor = lax.rsqrt(squares / D + EPS)
        normed = jnp.concatenate(kept, axis=1) * factor * s.gain[...]
        normed = normed.astype(BF16)

        slots, all_rows = buf("slots"), buf("all_rows")
        plane = [{}, {}, {}]
        for p in every:
            _, second, last = AXES[p]
            slots[p][at[second], at[last]] = normed[:, STARTS[p] : STARTS[p] + WIDTHS[p]]
        for step in (0, 1, 3, 2):
            for p in every:
                _, second, last = AXES[p]
                block = slots[p].at[at[second], at[last]]
                plane[p][step] = [
                    copies.start(
                        block,
                        block,
                        device_at(at, **{second: (at[second] + step) % 4, last: (at[last] + k) % 4}),
                    )
                    for k in (1, 3, 2, 0)
                    if step > 0 or k > 0
                ]
        yield
        third = [{}, {}, {}]

        def start3(p, step):
            first, second, _ = AXES[p]
            j = (at[second] + step) % 4
            for copy in plane[p][(4 - step) % 4]:
                copy.wait_recv()
            for m in range(4):
                s.blocks[p][pl.ds(NB * m, NB), :] = slots[p][j, m].astype(F32)
            all_rows[p][at[first], j] = s.blocks[p][...].astype(BF16)
            if step in DIRECT_GATHER:
                ring = GatherDirect(copies, lambda t: all_rows[p].at[t, j], at[first], three(first))
            else:
                ring = GatherRing(
                    copies, lambda t, cut: all_rows[p].at[t, j, :, pl.ds(*cut)], side(first), CUTS[p]
                )
            ring.start()
            third[p][step] = ring

        for step in (0, 3, 1, 2):
            for p in every:
                start3(p, step)
            if step == 1:
                for p in every:
                    third[p][0].middle()
        for step in (3, 1, 2):
            for p in every:
                third[p][step].middle()
        yield
        if f == 0:
            for load in loads[1:]:
                load.wait()
            for copy in traded:
                copy.wait_recv()
        row, col = iota((64 * NB, 64 * NB), 0), iota((64 * NB, 64 * NB), 1)
        for p in every:
            for step in (0, 3, 1, 2):
                third[p][step].near()
                third[p][step].far()
            rows = all_rows[p][...].reshape(64 * NB, WIDTHS[p])
            if p > 0:
                order = jnp.where(col == place(p, row), 1.0, 0.0).astype(BF16)
                rows = jnp.dot(order, rows, preferred_element_type=F32).astype(BF16)
            matrix = s.gates[:, :, pl.ds(STARTS[p], WIDTHS[p])].reshape(4 * FF_OWN, WIDTHS[p])
            product = lax.dot_general(matrix, rows, NT, preferred_element_type=F32)
            if p > 0:
                product += s.sums[...]
            s.sums[...] = product
        gate, up = s.sums[pl.ds(0, 2 * FF_OWN), :], s.sums[pl.ds(2 * FF_OWN, 2 * FF_OWN), :]
        s.turned[...] = (gate / (1.0 + jnp.exp(-gate)) * up).astype(BF16)

        parts, lasts = buf("parts"), buf("lasts")
        first = [[], [], []]

        def start1(p, k):
            j = (at[AXES[p][1]] + STEPS[k]) % 4
            axis = AXES[p][0]
            chunk = lambda t, cut: parts[p].at[k, t, :, pl.ds(*cut)]
            if k in DIRECT_SCATTER:
                ring = ScatterDirect(copies, chunk, buf("wholes")[p].at[k - RINGS], at[axis], three(axis), CUTS[p])
            else:
                ring = ScatterRing(
                    copies, chunk, buf("landings")[p].at[k], buf("passings")[p].at[k], side(axis), CUTS[p]
                )
            ring.start()
            first[p].append(ring)

        ending = [[], [], []]

        def end1(p, k):
            _, second, last = AXES[p]
            j = (at[second] + STEPS[k]) % 4
            for (start, size), value in zip(CUTS[p], first[p][k].end()):
                for m in range(4):
                    lasts[p][j, m, :, pl.ds(start, size)] = value[NB * m : NB * m + NB].astype(BF16)
            for step in (2, 1, 3, 0):
                if k < 3 or step > 0:
                    to = (at[last] + step) % 4
                    device = device_at(at, **{second: j, last: to})
                    landing = buf("landings3")[p].at[len(ending[p])]
                    ending[p].append(copies.start(lasts[p].at[j, to], landing, device))

        acts = []
        for p in every:
            k = row >> (LB + 4)
            step = jnp.where(k == 0, 2, jnp.where(k == 1, 1, jnp.where(k == 2, 3, 0)))
            lead = (row >> (LB + 2)) & 3
            middle = (step + at[AXES[p][1]]) & 3
            index = (lead * 4 + middle) * (4 * NB) + (row & (4 * NB - 1))
            order = jnp.where(index == place(p, col), 1.0, 0.0).astype(BF16)
            acts.append(lax.dot_general(order, s.turned[...], NT, preferred_element_type=F32).astype(BF16))
        for k in range(4):
            for p in every:
                for start, size in CUTS[p]:
                    matrix = s.downs[:, :, pl.ds(STARTS[p] + start, size)].reshape(2 * FF_OWN, size)
                    out = jnp.dot(
                        acts[p][16 * NB * k : 16 * NB * (k + 1)], matrix, preferred_element_type=F32
                    )
                    parts[p][k, :, :, pl.ds(start, size)] = out.reshape(4, 4 * NB, size).astype(BF16)
                if k < START_AHEAD:
                    start1(p, k)
        for k in range(4):
            yield
            for p in every:
                first[p][k].middle()
                if k + START_AHEAD < 4:
                    start1(p, k + START_AHEAD)
            if k >= LAG:
                for p in every:
                    end1(p, k - LAG)
        for k in range(4 - LAG, 4):
            yield
            for p in every:
                end1(p, k)
        yield
        for p in every:
            _, second, last = AXES[p]
            cols = pl.ds(STARTS[p], WIDTHS[p])
            total = buf("resid")[:, cols] + lasts[p][at[second], at[last]].astype(F32)
            for k in range(15):
                ending[p][k].wait_recv()
                total += buf("landings3")[p][k].astype(F32)
            out_ref[:, cols] = total.astype(BF16)
        yield

    early = []
    for b in range(SEQ):
        attend(b, b % 2)
        if b == 1:
            early = send_latents(0)
    for _ in flow(0):
        pass
    copies.finish()


def on_device(
    hidden_in, q_nope, q_rope, new_kv, cache_kv, lengths,
    w_uk, w_uv, w_out, norm_gain, w_gate, w_up, w_down,
):
    vmem = pl.BlockSpec(memory_space=pltpu.VMEM)
    hbm = pl.BlockSpec(memory_space=pl.ANY)
    return pl.pallas_call(
        layer_kernel,
        out_shape=jax.ShapeDtypeStruct((SEQ, D), BF16),
        in_specs=[pl.BlockSpec(memory_space=pltpu.SMEM)] + [vmem] * 5 + [hbm] * 7,
        out_specs=vmem,
        scratch_shapes=declare().shapes,
        compiler_params=pltpu.CompilerParams(
            collective_id=0, has_side_effects=True, vmem_limit_bytes=VMEM_LIMIT
        ),
        name="layer",
    )(
        lengths, q_nope, q_rope, new_kv, hidden_in, norm_gain.reshape(D // 128, 128),
        jnp.swapaxes(cache_kv, 1, 2), w_uk, w_uv, w_out, w_gate.T, w_up.T, w_down,
    )


def solution(mesh):
    return jax.shard_map(
        on_device,
        mesh=mesh,
        in_specs=(
            P(("rep", "grp"), None),
            P(("rep", "grp"), None),
            P(("rep", "grp"), None),
            P(("rep", "grp"), None),
            P(("rep", "grp"), None, None),
            P(("rep", "grp")),
            P("rep", None),
            P("rep", None),
            P("grp", None),
            P(),
            P(None, ("rep", "grp")),
            P(None, ("rep", "grp")),
            P(("rep", "grp"), None),
        ),
        out_specs=P(("rep", "grp"), None),
        check_vma=False,
    )
```

time: 767 us -> 110 us (0.14)
  waiting for transfers between devices: 663 us -> 0 us
  Pallas kernels: 0 us -> 109 us
  matrix products: 48.1 us -> 0 us
  local copies, waits for them, and re-layouts: 18.3 us -> 1.46 us
  other arithmetic: 15.2 us -> 0 us
  between operations: 13.3 us -> 0.01 us
  starting transfers between devices: 7.71 us -> 0 us
    psum x1 -> x0, waiting for transfers between devices: 310 us -> none  [on_device(): summed = lax.psum(partial_value.astype(jnp.bfloat16), 'grp')]
    unnamed x5 -> x0, waiting for transfers between devices: 174 us -> none
    all_gather x2 -> x0, waiting for transfers between devices: 170 us -> none  [the longest x1 114 us: in_one_piece(): lax.all_gather(both, axis, axis=dim, tiled=True)]
    pallas_call x0 -> x1, Pallas kernels: none -> 109 us  [on_device(): pl.pallas_call(layer_kernel, out_shape=jax.ShapeDtypeStruct((SEQ, D), BF1...]
    dot_general x8 -> x0, matrix products: 48.1 us -> none  [the longest x1 13.5 us: on_device(): jnp.dot(activated, w_down, preferred_element_type=jnp.float32)]
    split x1 -> x0, local copies, waits for them, and re-layouts: 9.07 us -> none  [in_one_piece(): jnp.split(lax.all_gather(both, axis, axis=dim, tiled=True), ends, axis=al...]
    all_to_all x1 -> x0, waiting for transfers between devices: 8.28 us -> none  [on_device(): lax.all_to_all(head_out, 'grp', split_axis=1, concat_axis=0, tiled=True)]
  transfers between devices with their start and end apart: 5 -> 0, of which waited for: 5 -> 0; matrix products, arithmetic and copies ran while one was open for 0% -> 0% of each run, Pallas kernels for 0% -> 0%
where the time goes in v3:
time: 110 us
  Pallas kernels  109 us (99%)
  local copies, waits for them, and re-layouts  1.46 us (1%)
    pallas_call x1, Pallas kernels, on_device(): pl.pallas_call(layer_kernel, out_shape=jax.ShapeDtypeStruct((SEQ, D), BF1...  109 us

profile of v3, /device:TPU:0, one launch (start us, length us, event | category | flops | bytes accessed | tf_op | source)
XLA Modules:
  0.0 110.2 jit_solution(5301260077891041454)
XLA Ops:
  0.0 108.8 %layer.1 = bf16[4,7168]{1,0:T(4,128)(2,1)} custom-call(s32[4]{0:T(128)} %len_ref.1, bf16[4,8192]{1,0:T(4,128)(2,1)} %q_ref.1, bf16[4,4096]{1,0:T(4,128)(2,1)} %rope_ref.1, bf16[4,576]{1,0:T(4,128)(2,1)} %new_ref.1, bf16[4,7168]{1,0:T(4,128)(2,1)} %hidden_ref.1, bf16[56,128]{1,0:T(8,128)(2,1)} %bitcast.7, bf16[4,576,4096]{2,1,0:T(8,128)(2,1)} %bitcast.4, ...), custom_call_target="tpu_custom_call" | custom-call | tf_op jit(solution)/shard_map/layer/pallas_call | solution.py:718
  108.8 1.5 %copy.15 = bf16[4,7168]{1,0:T(4,128)(2,1)} copy(bf16[4,7168]{1,0:T(4,128)(2,1)} %layer.1) | data formatting | bytes 114688

commit v4 on v3

--- a/solution.py
+++ b/solution.py
@@ -570,7 +570,7 @@
                         block,
                         device_at(at, **{second: (at[second] + step) % 4, last: (at[last] + k) % 4}),
                     )
-                    for k in (1, 3, 2, 0)
+                    for k in (2, 1, 3, 0)
                     if step > 0 or k > 0
                 ]
         yield
@@ -665,16 +665,18 @@
             index = (lead * 4 + middle) * (4 * NB) + (row & (4 * NB - 1))
             order = jnp.where(index == place(p, col), 1.0, 0.0).astype(BF16)
             acts.append(lax.dot_general(order, s.turned[...], NT, preferred_element_type=F32).astype(BF16))
-        for k in range(4):
+        for k in (0, 2):
             for p in every:
                 for start, size in CUTS[p]:
                     matrix = s.downs[:, :, pl.ds(STARTS[p] + start, size)].reshape(2 * FF_OWN, size)
                     out = jnp.dot(
-                        acts[p][16 * NB * k : 16 * NB * (k + 1)], matrix, preferred_element_type=F32
+                        acts[p][16 * NB * k : 16 * NB * (k + 2)], matrix, preferred_element_type=F32
                     )
-                    parts[p][k, :, :, pl.ds(start, size)] = out.reshape(4, 4 * NB, size).astype(BF16)
-                if k < START_AHEAD:
-                    start1(p, k)
+                    out = out.reshape(2, 4, 4 * NB, size).astype(BF16)
+                    parts[p][pl.ds(k, 2), :, :, pl.ds(start, size)] = out
+                for one in (k, k + 1):
+                    if one < START_AHEAD:
+                        start1(p, one)
         for k in range(4):
             yield
             for p in every:

time: 110 us -> 109 us (level)
  Pallas kernels: 109 us -> 107 us
    pallas_call x1, Pallas kernels: 109 us -> 107 us  [on_device(): pl.pallas_call(layer_kernel, out_shape=jax.ShapeDtypeStruct((SEQ, D), BF1...]
where the time goes in v4:
time: 109 us
  Pallas kernels  107 us (98%)
  local copies, waits for them, and re-layouts  1.46 us (1%)
    pallas_call x1, Pallas kernels, on_device(): pl.pallas_call(layer_kernel, out_shape=jax.ShapeDtypeStruct((SEQ, D), BF1...  107 us

profile of v4, /device:TPU:0, one launch (start us, length us, event | category | flops | bytes accessed | tf_op | source)
XLA Modules:
  0.0 108.6 jit_solution(1006911473671867931)
XLA Ops:
  0.0 107.1 %layer.1 = bf16[4,7168]{1,0:T(4,128)(2,1)} custom-call(s32[4]{0:T(128)} %len_ref.1, bf16[4,8192]{1,0:T(4,128)(2,1)} %q_ref.1, bf16[4,4096]{1,0:T(4,128)(2,1)} %rope_ref.1, bf16[4,576]{1,0:T(4,128)(2,1)} %new_ref.1, bf16[4,7168]{1,0:T(4,128)(2,1)} %hidden_ref.1, bf16[56,128]{1,0:T(8,128)(2,1)} %bitcast.7, bf16[4,576,4096]{2,1,0:T(8,128)(2,1)} %bitcast.4, ...), custom_call_target="tpu_custom_call" | custom-call | tf_op jit(solution)/shard_map/layer/pallas_call | solution.py:720
  107.1 1.5 %copy.15 = bf16[4,7168]{1,0:T(4,128)(2,1)} copy(bf16[4,7168]{1,0:T(4,128)(2,1)} %layer.1) | data formatting | bytes 114688
